TPU v7x, 256 devices: a whole 4x4x8 slice. The times are simulated.
256 devices in a mesh: gx: 4 (over y_lo, core), gz: 8 (over y_hi, x), ta: 8 (over z).
Axes of the slice: x: 4, y: 4 (y_hi: 2, y_lo: 2; y = y_hi * 2 + y_lo), z: 8, core: 2. Of those that a mesh axis runs over, the one named last changes fastest.
Arguments:
- links: float32 [4, 2, 3, 3, 32, 32, 512], P(None, None, None, None, 'ta', 'gz', 'gx'), may hold values from -1 to 1, as said below
Outputs:
- force: float32 [4, 2, 3, 3, 32, 32, 512], P(None, None, None, None, 'ta', 'gz', 'gx')
Inputs may be any that keep to these rules, and one draw needn't show every extreme that they name: Every link matrix (real part links[mu, 0], imaginary part links[mu, 1]) is special unitary, up to float32 rounding.
All inputs are finite; a program needn't handle non-finite values.
Results may differ from a plain program's by a relative error of at most 0.0003.
Values sent between devices are 32-bit elements; how exact they have to be, the bound alone decides.
A program may use at most 64 MiB of HBM per device.

v0:
```python
import jax
import jax.numpy as jnp
from jax import lax
from jax.sharding import PartitionSpec as P

NX = 16


COEFF = -1.9


def padded(block, sides, width):
    for axis, dim in sides:
        count = lax.axis_size(axis)
        forward = [(i, i + 1) for i in range(count - 1)]
        forward.append((count - 1, 0))
        backward = [(target, source) for source, target in forward]
        low = lax.ppermute(
            lax.slice_in_dim(block, block.shape[dim] - width, None, axis=dim), axis, forward
        )
        high = lax.ppermute(lax.slice_in_dim(block, 0, width, axis=dim), axis, backward)
        block = jnp.concatenate([low, block, high], axis=dim)
    return block


def matprod(left, right):
    total = left[:, 0][:, None] * right[0][None, :]
    total = total + left[:, 1][:, None] * right[1][None, :]
    return total + left[:, 2][:, None] * right[2][None, :]


def complex_mul(left, right):
    return (
        matprod(left[0], right[0]) - matprod(left[1], right[1]),
        matprod(left[0], right[1]) + matprod(left[1], right[0]),
    )


def dagger(matrix):
    return (jnp.swapaxes(matrix[0], 0, 1), -jnp.swapaxes(matrix[1], 0, 1))


def unit_step(direction, sign):
    offset = [0, 0, 0, 0]
    offset[direction] = sign
    return tuple(offset)


def joined(first_step, second_step):
    return tuple((first_step[position] + second_step[position] for position in range(4)))


def gauge_force(fetch_link):
    blocks = []
    still = (0, 0, 0, 0)
    for direction in range(4):
        ahead = unit_step(direction, 1)
        summed = None
        for transverse in range(4):
            if transverse == direction:
                continue
            side_up = unit_step(transverse, 1)
            side_down = unit_step(transverse, -1)
            upper = complex_mul(
                complex_mul(fetch_link(transverse, ahead), dagger(fetch_link(direction, side_up))),
                dagger(fetch_link(transverse, still)),
            )
            lower = complex_mul(
                complex_mul(
                    dagger(fetch_link(transverse, joined(ahead, side_down))),
                    dagger(fetch_link(direction, side_down)),
                ),
                fetch_link(transverse, side_down),
            )
            staple = (upper[0] + lower[0], upper[1] + lower[1])
            summed = staple if summed is None else (summed[0] + staple[0], summed[1] + staple[1])
        loop_matrix = complex_mul(fetch_link(direction, still), summed)
        real_part = 0.5 * (loop_matrix[0] - jnp.swapaxes(loop_matrix[0], 0, 1))
        imag_part = 0.5 * (loop_matrix[1] + jnp.swapaxes(loop_matrix[1], 0, 1))
        trace_third = (loop_matrix[1][0, 0] + loop_matrix[1][1, 1] + loop_matrix[1][2, 2]) / 3.0
        identity = jnp.eye(3, dtype=jnp.float32).reshape((3, 3) + (1,) * trace_third.ndim)
        imag_part = imag_part - identity * trace_third
        blocks.append(COEFF * jnp.stack([real_part, imag_part], axis=0))
    return jnp.stack(blocks, axis=0)


def complete_rows(wider):
    real0 = wider[:, 0, 0]
    imag0 = wider[:, 1, 0]
    real1 = wider[:, 0, 1]
    imag1 = wider[:, 1, 1]
    real_cols = []
    imag_cols = []
    for column in range(3):
        next_col = (column + 1) % 3
        last_col = (column + 2) % 3
        cross_real = (
            real0[:, next_col] * real1[:, last_col]
            - imag0[:, next_col] * imag1[:, last_col]
            - real0[:, last_col] * real1[:, next_col]
            + imag0[:, last_col] * imag1[:, next_col]
        )
        cross_imag = (
            real0[:, next_col] * imag1[:, last_col]
            + imag0[:, next_col] * real1[:, last_col]
            - real0[:, last_col] * imag1[:, next_col]
            - imag0[:, last_col] * real1[:, next_col]
        )
        real_cols.append(cross_real)
        imag_cols.append(-cross_imag)
    third = jnp.stack([jnp.stack(real_cols, axis=1), jnp.stack(imag_cols, axis=1)], axis=1)
    return jnp.concatenate([wider, third[:, :, None]], axis=2)


def per_device(links):
    payload = links[:, :, 0:2]
    wider = padded(payload, (("gx", 6),), NX)
    wider = padded(wider, (("ta", 4), ("gz", 5)), 1)
    wider = complete_rows(wider)
    time_len = links.shape[4]
    depth_len = links.shape[5]
    flat_len = links.shape[6]
    column = lax.broadcasted_iota(jnp.int32, (flat_len,), 0) % NX
    right_edge = column == NX - 1
    left_edge = column == 0

    def fetch_link(direction, offset):
        start = NX + offset[2] * NX
        field = wider[
            direction,
            :,
            :,
            :,
            1 + offset[0] : 1 + offset[0] + time_len,
            1 + offset[1] : 1 + offset[1] + depth_len,
            start : start + flat_len,
        ]
        if offset[3] == 1:
            field = jnp.where(
                right_edge, jnp.roll(field, NX - 1, axis=5), jnp.roll(field, -1, axis=5)
            )
        elif offset[3] == -1:
            field = jnp.where(
                left_edge, jnp.roll(field, 1 - NX, axis=5), jnp.roll(field, 1, axis=5)
            )
        return (field[0], field[1])

    return gauge_force(fetch_link)


def solution(mesh):
    return jax.shard_map(
        per_device,
        mesh=mesh,
        in_specs=(P(None, None, None, None, "ta", "gz", "gx"),),
        out_specs=P(None, None, None, None, "ta", "gz", "gx"),
        check_vma=False,
    )
```

profile of v0, /device:TPU:14, one launch (start us, length us, event | category | flops | bytes accessed | tf_op | source)
XLA Modules:
  0.0 70.3 jit_solution(11727214759005900719)
XLA Ops:
  0.0 1.4 %fusion.22 = (f32[4,2,2,3,4,4,16]{6,5,4,3,2,1,0:T(4,128)S(1)}, f32[4,2,2,3,4,4,16]{6,5,4,3,2,1,0:T(4,128)S(1)}) fusion(f32[4,2,3,3,4,4,128]{6,5,4,3,2,1,0:T(4,128)} %param.1), kind=kLoop, calls=%fused_computation.729 | loop fusion | bytes 196608 | tf_op jit(solution)/shard_map/slice | solution.py:19
  1.4 0.3 copy.21
  1.8 0.3 copy.19
  2.1 0.6 collective-permute-start
  2.6 0.3 copy.20
  2.9 7.2 %collective-permute-done.1 = f32[4,2,2,3,4,4,16]{6,0,5,4,3,2,1:T(4,128)S(1)} collective-permute-done((f32[4,2,2,3,4,4,16]{6,0,5,4,3,2,1:T(4,128)S(1)}, f32[4,2,2,3,4,4,16]{6,0,5,4,3,2,1:T(4,128)S(1)}, u32[]{:S(2)}, u32[]{:S(2)}) %collective-permute-start.1) | collective-permute-done | bytes 49184 | tf_op jit(solution)/shard_map/ppermute | solution.py:21
  10.1 3.1 %collective-permute-done = f32[4,2,2,3,4,4,16]{6,0,5,4,3,2,1:T(4,128)S(1)} collective-permute-done((f32[4,2,2,3,4,4,16]{6,0,5,4,3,2,1:T(4,128)S(1)}, f32[4,2,2,3,4,4,16]{6,0,5,4,3,2,1:T(4,128)S(1)}, u32[]{:S(2)}, u32[]{:S(2)}) %collective-permute-start) | collective-permute-done | bytes 49184 | tf_op jit(solution)/shard_map/ppermute | solution.py:18
  13.2 0.4 pad_maximum_fusion.10
  13.6 2.0 %collective-permute-start.2 = (f32[4,2,2,3,1,4,160]{6,0,5,4,3,2,1:T(4,128)S(1)}, f32[4,2,2,3,1,4,160]{6,0,5,4,3,2,1:T(4,128)S(1)}, u32[]{:S(2)}, u32[]{:S(2)}) collective-permute-start(f32[4,2,2,3,1,4,160]{6,0,5,4,3,2,1:T(4,128)S(1)} %get-tuple-element.90), channel_id=1, source_target_pairs={{0,1},{1,2},{2,3},{3,4},{4,5},{5,6},{6,7},{7,0},{8,9},{9,10},{10,1... | collective-permute-start | bytes 368648 | tf_op jit(solution)/shard_map/ppermute | solution.py:18
  15.6 4.0 %collective-permute-start.3 = (f32[4,2,2,3,1,4,160]{6,0,5,4,3,2,1:T(4,128)S(1)}, f32[4,2,2,3,1,4,160]{6,0,5,4,3,2,1:T(4,128)S(1)}, u32[]{:S(2)}, u32[]{:S(2)}) collective-permute-start(f32[4,2,2,3,1,4,160]{6,0,5,4,3,2,1:T(4,128)S(1)} %get-tuple-element.91), channel_id=1, source_target_pairs={{1,0},{2,1},{3,2},{4,3},{5,4},{6,5},{7,6},{0,7},{9,8},{10,9},{11,1... | collective-permute-start | bytes 368648 | tf_op jit(solution)/shard_map/ppermute | solution.py:21
  19.6 4.7 %collective-permute-done.2 = f32[4,2,2,3,1,4,160]{6,0,5,4,3,2,1:T(4,128)S(1)} collective-permute-done((f32[4,2,2,3,1,4,160]{6,0,5,4,3,2,1:T(4,128)S(1)}, f32[4,2,2,3,1,4,160]{6,0,5,4,3,2,1:T(4,128)S(1)}, u32[]{:S(2)}, u32[]{:S(2)}) %collective-permute-start.2) | collective-permute-done | bytes 122912 | tf_op jit(solution)/shard_map/ppermute | solution.py:18
  24.4 0.4 pad_maximum_fusion.7
  24.7 2.1 %collective-permute-start.4 = (f32[4,2,2,3,6,1,160]{6,0,5,4,3,2,1:T(4,128)S(1)}, f32[4,2,2,3,6,1,160]{6,0,5,4,3,2,1:T(4,128)S(1)}, u32[]{:S(2)}, u32[]{:S(2)}) collective-permute-start(f32[4,2,2,3,6,1,160]{6,0,5,4,3,2,1:T(4,128)S(1)} %get-tuple-element.84), channel_id=1, source_target_pairs={{0,8},{8,16},{16,24},{24,32},{32,40},{40,48},{48,56},{56,0},{1,9},... | collective-permute-start | bytes 552968 | tf_op jit(solution)/shard_map/ppermute | solution.py:18
  26.9 0.3 pad_maximum_fusion.20
  27.2 5.7 %collective-permute-done.4 = f32[4,2,2,3,6,1,160]{6,0,5,4,3,2,1:T(4,128)S(1)} collective-permute-done((f32[4,2,2,3,6,1,160]{6,0,5,4,3,2,1:T(4,128)S(1)}, f32[4,2,2,3,6,1,160]{6,0,5,4,3,2,1:T(4,128)S(1)}, u32[]{:S(2)}, u32[]{:S(2)}) %collective-permute-start.4) | collective-permute-done | bytes 184352 | tf_op jit(solution)/shard_map/ppermute | solution.py:18
  32.9 5.2 %collective-permute-done.5 = f32[4,2,2,3,6,1,160]{6,0,5,4,3,2,1:T(4,128)S(1)} collective-permute-done((f32[4,2,2,3,6,1,160]{6,0,5,4,3,2,1:T(4,128)S(1)}, f32[4,2,2,3,6,1,160]{6,0,5,4,3,2,1:T(4,128)S(1)}, u32[]{:S(2)}, u32[]{:S(2)}) %collective-permute-start.5) | collective-permute-done | bytes 184352 | tf_op jit(solution)/shard_map/ppermute | solution.py:21
  38.1 1.1 %pad_maximum_fusion.1 = f32[4,2,2,3,6,6,160]{6,0,5,4,3,2,1:T(4,128)S(1)} fusion(f32[4,2,2,3,6,1,160]{6,0,5,4,3,2,1:T(4,128)S(1)} %collective-permute-done.5, f32[4,2,2,3,1,4,160]{6,0,5,4,3,2,1:T(4,128)S(1)} %collective-permute-done.3, f32[4,2,2,3,4,4,16]{6,0,5,4,3,2,1:T(4,128)S(1)} %collective-permute-done.1, f32[4,2,2,3,4,4,128]{6,0,5,4,3,2,1:T(4,128)S(1)} %copy.20, ...), kind=kLoop, calls=%fused_computation.1 | loop fusion | flops 1658880 | bytes 2211840 | tf_op jit(solution)/shard_map/concatenate | solution.py:22
  39.3 0.3 slice_bitcast_fusion.2
  39.6 0.2 multiply_add_fusion.1
  39.8 0.2 multiply_add_fusion.2
  40.0 0.2 subtract_negate_fusion.2
  40.2 0.2 maximum_bitcast_fusion.1
  40.5 0.2 maximum_bitcast_fusion
  40.7 0.3 fusion.21
  41.0 1.5 %pad_maximum_fusion = f32[4,2,3,3,6,6,160]{6,0,5,4,3,2,1:T(4,128)S(1)} fusion(f32[4,2,1,3,6,6,160]{6,0,5,4,3,2,1:T(4,128)S(1)} %maximum_bitcast_fusion, f32[4,2,2,3,6,1,160]{6,0,5,4,3,2,1:T(4,128)S(1)} %collective-permute-done.5, f32[4,2,2,3,1,4,160]{6,0,5,4,3,2,1:T(4,128)S(1)} %collective-permute-done.3, ...), kind=kLoop, calls=%fused_computation | loop fusion | flops 2903040 | bytes 3317760 | tf_op jit(solution)/shard_map/concatenate | solution.py:112
  42.5 2.5 %slice_negate_fusion.23 = (f32[1,1,3,3,4,4,128]{6,0,5,4,3,2,1:T(1,128)S(1)}, f32[1,1,3,3,4,4,128]{6,0,5,4,3,2,1:T(1,128)S(1)}, f32[1,1,3,3,4,4,128]{6,0,5,4,3,2,...) fusion(f32[4,2,3,3,6,6,160]{6,0,5,4,3,2,1:T(4,128)S(1)} %pad_ma, ...), kind=kLoop, calls=%fused_computation.85 | loop fusion | flops 55296 | bytes 2654208 | tf_op jit(solution)/shard_map/neg | solution.py:40
  45.2 2.7 %fusion.18 = (f32[1,1,3,3,4,4,128]{6,0,5,4,3,2,1:T(1,128)S(1)}, f32[1,1,3,3,4,4,128]{6,0,5,4,3,2,1:T(1,128)S(1)}, f32[1,1,3,3,4,4,128]{6,0,5,4,3,2,1:T(1,128)S(1...) fusion(f32[4,2,3,3,6,6,160]{6,0,5,4,3,2,1:T(4,128)S(1)} %pad_ma, ...), kind=kLoop, calls=%fused_computation.725 | loop fusion | flops 147456 | bytes 2801664 | tf_op jit(solution)/shard_map/slice | solution.py:146
  48.0 2.5 %fusion.19 = (f32[1,1,3,3,4,4,128]{6,0,5,4,3,2,1:T(1,128)S(1)}, f32[1,1,3,3,4,4,128]{6,0,5,4,3,2,1:T(1,128)S(1)}, f32[1,1,3,3,4,4,128]{6,0,5,4,3,2,1:T(1,128)S(1...) fusion(f32[4,2,3,3,6,6,160]{6,0,5,4,3,2,1:T(4,128)S(1)} %pad_ma, ...), kind=kLoop, calls=%fused_computation.726 | loop fusion | flops 73728 | bytes 2801664 | tf_op jit(solution)/shard_map/slice | solution.py:146
  50.5 2.9 %fusion.20 = (f32[1,2,3,3,4,4,128]{6,0,5,4,3,2,1:T(1,128)S(1)}, f32[1,2,3,3,4,4,128]{6,0,5,4,3,2,1:T(1,128)S(1)}, f32[1,2,3,3,4,4,128]{6,0,5,4,3,2,1:T(1,128)S(1...) fusion(f32[4,2,3,3,6,6,160]{6,0,5,4,3,2,1:T(4,128)S(1)} %pad_ma, ...), kind=kLoop, calls=%fused_computation.727 | loop fusion | bytes 2949120 | tf_op jit(solution)/shard_map/slice | solution.py:129
  53.8 0.1 slice.4514
  54.0 0.1 slice.4120
  54.3 0.1 slice.4450
  54.8 0.4 slice.4148
  55.9 0.1 fusion.32
  56.0 0.1 fusion.31
  56.2 0.1 fusion.34
  56.3 0.1 fusion.33
  56.5 0.1 fusion.28
  56.6 0.1 fusion.27
  56.8 0.1 fusion.30
  56.9 0.1 fusion.29
  57.1 0.1 fusion.24
  57.2 0.1 fusion.23
  57.4 0.1 fusion.26
  57.5 0.1 fusion.25
  57.7 0.7 maximum_select_fusion
  60.8 0.4 maximum_select_fusion.11
  61.5 0.5 maximum_select_fusion.6
  62.3 0.7 maximum_select_fusion.1
  64.0 0.2 pad_maximum_fusion.28
  64.2 0.3 pad_maximum_fusion.21
  64.5 0.4 add_add_fusion.2
  64.9 0.4 add_add_fusion.1
  65.4 0.4 add_add_fusion.10
  65.9 0.4 add_add_fusion.11
  66.4 0.2 multiply_bitcast_fusion
  66.5 0.2 multiply_bitcast_fusion.1
  66.8 0.4 add_add_fusion.29
  67.2 0.4 add_add_fusion.28
  67.7 0.2 multiply_bitcast_fusion.3
  68.0 0.4 add_add_fusion.20
  68.4 0.4 add_add_fusion.19
  68.9 0.2 multiply_bitcast_fusion.2
  69.3 0.9 %pad_maximum_fusion.2 = f32[4,2,3,3,4,4,128]{6,5,4,3,2,1,0:T(4,128)} fusion(f32[1,2,3,3,4,4,128]{6,5,4,3,2,1,0:T(4,128)S(1)} %maximum_multiply_fusion.3, f32[1,2,3,3,4,4,128]{6,5,4,3,2,1,0:T(4,128)S(1)} %maximum_multiply_fusion.2, f32[1,2,3,3,4,4,128]{6,5,4,3,2,1,0:T(4,128)S(1)} %maximum_multiply_fusion.1, ...), kind=kLoop, calls=%fused_computation.3 | loop fusion | flops 442368 | bytes 1179648 | tf_op jit(solution)/shard_map/stack | solution.py:84
  (251 shorter events, 5.3 us)
Async XLA Ops:
  0.0 2.6 %slice-start = ((f32[4,2,3,3,4,4,128]{6,5,4,3,2,1,0:T(4,128)}), f32[4,2,2,3,4,4,128]{6,5,4,3,2,1,0:T(4,128)S(1)}, s32[]{:S(2)}) async-start(f32[4,2,3,3,4,4,128]{6,5,4,3,2,1,0:T(4,128)} %param.1), calls=%async_computation | async-start | bytes 786432 | tf_op jit(solution)/shard_map/slice | solution.py:116
  1.7 8.4 %collective-permute-start.1 = (f32[4,2,2,3,4,4,16]{6,0,5,4,3,2,1:T(4,128)S(1)}, f32[4,2,2,3,4,4,16]{6,0,5,4,3,2,1:T(4,128)S(1)}, u32[]{:S(2)}, u32[]{:S(2)}) collective-permute-start(f32[4,2,2,3,4,4,16]{6,0,5,4,3,2,1:T(4,128)S(1)} %copy.21), channel_id=1, source_target_pairs={{64,0},{128,64},{192,128},{0,192},{65,1},{129,65},{193,129},{1,193... | collective-permute-start | bytes 147464 | tf_op jit(solution)/shard_map/ppermute | solution.py:21
  2.1 11.2 %collective-permute-start = (f32[4,2,2,3,4,4,16]{6,0,5,4,3,2,1:T(4,128)S(1)}, f32[4,2,2,3,4,4,16]{6,0,5,4,3,2,1:T(4,128)S(1)}, u32[]{:S(2)}, u32[]{:S(2)}) collective-permute-start(f32[4,2,2,3,4,4,16]{6,0,5,4,3,2,1:T(4,128)S(1)} %copy.19), channel_id=1, source_target_pairs={{0,64},{64,128},{128,192},{192,0},{1,65},{65,129},{129,193},{193,1... | collective-permute-start | bytes 147464 | tf_op jit(solution)/shard_map/ppermute | solution.py:18
  13.6 10.8 %collective-permute-start.2 = (f32[4,2,2,3,1,4,160]{6,0,5,4,3,2,1:T(4,128)S(1)}, f32[4,2,2,3,1,4,160]{6,0,5,4,3,2,1:T(4,128)S(1)}, u32[]{:S(2)}, u32[]{:S(2)}) collective-permute-start(f32[4,2,2,3,1,4,160]{6,0,5,4,3,2,1:T(4,128)S(1)} %get-tuple-element.90), channel_id=1, source_target_pairs={{0,1},{1,2},{2,3},{3,4},{4,5},{5,6},{6,7},{7,0},{8,9},{9,10},{10,1... | collective-permute-start | bytes 368648 | tf_op jit(solution)/shard_map/ppermute | solution.py:18
  15.6 8.8 %collective-permute-start.3 = (f32[4,2,2,3,1,4,160]{6,0,5,4,3,2,1:T(4,128)S(1)}, f32[4,2,2,3,1,4,160]{6,0,5,4,3,2,1:T(4,128)S(1)}, u32[]{:S(2)}, u32[]{:S(2)}) collective-permute-start(f32[4,2,2,3,1,4,160]{6,0,5,4,3,2,1:T(4,128)S(1)} %get-tuple-element.91), channel_id=1, source_target_pairs={{1,0},{2,1},{3,2},{4,3},{5,4},{6,5},{7,6},{0,7},{9,8},{10,9},{11,1... | collective-permute-start | bytes 368648 | tf_op jit(solution)/shard_map/ppermute | solution.py:21
  24.7 8.2 %collective-permute-start.4 = (f32[4,2,2,3,6,1,160]{6,0,5,4,3,2,1:T(4,128)S(1)}, f32[4,2,2,3,6,1,160]{6,0,5,4,3,2,1:T(4,128)S(1)}, u32[]{:S(2)}, u32[]{:S(2)}) collective-permute-start(f32[4,2,2,3,6,1,160]{6,0,5,4,3,2,1:T(4,128)S(1)} %get-tuple-element.84), channel_id=1, source_target_pairs={{0,8},{8,16},{16,24},{24,32},{32,40},{40,48},{48,56},{56,0},{1,9},... | collective-permute-start | bytes 552968 | tf_op jit(solution)/shard_map/ppermute | solution.py:18
  26.9 11.3 %collective-permute-start.5 = (f32[4,2,2,3,6,1,160]{6,0,5,4,3,2,1:T(4,128)S(1)}, f32[4,2,2,3,6,1,160]{6,0,5,4,3,2,1:T(4,128)S(1)}, u32[]{:S(2)}, u32[]{:S(2)}) collective-permute-start(f32[4,2,2,3,6,1,160]{6,0,5,4,3,2,1:T(4,128)S(1)} %get-tuple-element.85), channel_id=1, source_target_pairs={{8,0},{16,8},{24,16},{32,24},{40,32},{48,40},{56,48},{0,56},{9,1},... | collective-permute-start | bytes 552968 | tf_op jit(solution)/shard_map/ppermute | solution.py:21
where the time goes:
time: 70.4 us; the launch traced here: 70.3 us
  waiting for transfers between devices  26 us (37%)
  other arithmetic  22.5 us (32%)
  local copies, waits for them, and re-layouts  10.9 us (15%)
  starting transfers between devices  8.8 us (12%)
  between operations  2.04 us (3%)
    ppermute x3, waiting for transfers between devices, padded(): lax.ppermute(lax.slice_in_dim(block, block.shape[dim] - width, None, axis...  13.6 us
    ppermute x3, waiting for transfers between devices, padded(): lax.ppermute(lax.slice_in_dim(block, 0, width, axis=dim), axis, backward)  12.4 us
    slice x2, other arithmetic, fetch_link(): return (field[0], field[1])  5.21 us
    ppermute x3, starting transfers between devices, padded(): lax.ppermute(lax.slice_in_dim(block, block.shape[dim] - width, None, axis...  4.68 us
    ppermute x3, starting transfers between devices, padded(): lax.ppermute(lax.slice_in_dim(block, 0, width, axis=dim), axis, backward)  4.11 us
    slice x1, local copies, waits for them, and re-layouts, fetch_link(): wider[direction, :, :, :, 1 + offset[0]:1 + offset[0] + time_len, 1 + off...  2.89 us
    neg x17, other arithmetic, dagger(): return (jnp.swapaxes(matrix[0], 0, 1), -jnp.swapaxes(matrix[1], 0, 1))  2.77 us
    slice x10, local copies, waits for them, and re-layouts, fetch_link(): jnp.roll(field, 1, axis=5)  1.66 us
  transfers between devices with their start and end apart: 6, of which 5 were waited for; matrix products, arithmetic and copies ran while one was open for 1% of the time, Pallas kernels for 0%

commit v1 on v0

v1 whole, which is shorter than its diff:
```python
import jax
import jax.numpy as jnp
from jax import lax
from jax.experimental import pallas as pl
from jax.experimental.pallas import tpu as pltpu
from jax.sharding import PartitionSpec as P

COEFF = -1.9
MESH = pl.DeviceIdType.MESH
AXES = ("ta", "gz", "gx")
ROWS2 = 12
FULL = 18
CORNERS = ((0, 1), (0, 2), (1, 0), (1, 2), (2, 0), (2, 1))


def rs(v, k):
    k = k % 8
    return v if k == 0 else pltpu.roll(v, k, axis=0)


def rl(v, k):
    k = k % 128
    return v if k == 0 else pltpu.roll(v, k, axis=1)


def sublane():
    return lax.broadcasted_iota(jnp.int32, (8, 128), 0)


def lanes():
    return lax.broadcasted_iota(jnp.int32, (8, 128), 1)


def total(terms):
    out = terms[0]
    for t in terms[1:]:
        out = out + t
    return out


def mul_nn(a, b):
    return [
        [
            (
                total([a[i][k][0] * b[k][j][0] for k in range(3)])
                - total([a[i][k][1] * b[k][j][1] for k in range(3)]),
                total([a[i][k][0] * b[k][j][1] for k in range(3)])
                + total([a[i][k][1] * b[k][j][0] for k in range(3)]),
            )
            for j in range(3)
        ]
        for i in range(3)
    ]


def mul_hn(a, b):
    return [
        [
            (
                total([a[k][i][0] * b[k][j][0] for k in range(3)])
                + total([a[k][i][1] * b[k][j][1] for k in range(3)]),
                total([a[k][i][0] * b[k][j][1] for k in range(3)])
                - total([a[k][i][1] * b[k][j][0] for k in range(3)]),
            )
            for j in range(3)
        ]
        for i in range(3)
    ]


def mul_nh(a, b):
    return [
        [
            (
                total([a[i][k][0] * b[j][k][0] for k in range(3)])
                + total([a[i][k][1] * b[j][k][1] for k in range(3)]),
                total([a[i][k][1] * b[j][k][0] for k in range(3)])
                - total([a[i][k][0] * b[j][k][1] for k in range(3)]),
            )
            for j in range(3)
        ]
        for i in range(3)
    ]


def third_row(m):
    row = []
    for col in range(3):
        n, q = (col + 1) % 3, (col + 2) % 3
        r0n, i0n = m[0][n]
        r0q, i0q = m[0][q]
        r1n, i1n = m[1][n]
        r1q, i1q = m[1][q]
        row.append(
            (
                (r0n * r1q - i0n * i1q) - (r0q * r1n - i0q * i1n),
                (r0q * i1n + i0q * r1n) - (r0n * i1q + i0n * r1q),
            )
        )
    return row


def gather(entry, rows=3):
    return [[(entry(i * 6 + j), entry(i * 6 + 3 + j)) for j in range(3)] for i in range(rows)]


def scatter(put, m, first=0):
    for i, row in enumerate(m):
        for j, (re, im) in enumerate(row):
            put((first + i) * 6 + j, re)
            put((first + i) * 6 + 3 + j, im)


def kernel(
    x_hbm, o_hbm, u, v, p, l, s, a, o,
    sft, sbt, sfz, sbz, sfy, sby, sc,
    hft, hbt, hfz, hbz, hfy, hby, hc, lt, lz, ly,
    in_sem, out_sem, send_sem, recv_sem,
):
    me = {axis: lax.axis_index(axis) for axis in AXES}
    size = {axis: lax.axis_size(axis) for axis in AXES}

    def at(steps):
        return {
            AXES[d]: lax.rem(me[AXES[d]] + (step + size[AXES[d]]), size[AXES[d]])
            for d, step in steps
        }

    barrier = pltpu.get_barrier_semaphore()
    targets = [at(((d, sgn),)) for d in range(3) for sgn in (-1, 1)]
    targets += [at(((back, 1), (ahead, -1))) for back, ahead in CORNERS]
    for target in targets:
        pl.semaphore_signal(barrier, inc=1, device_id=target, device_id_type=MESH)

    loads = [pltpu.make_async_copy(x_hbm.at[d], u.at[d], in_sem.at[d]) for d in range(4)]
    for load in loads:
        load.start()
    for load in loads:
        load.wait()

    def link(d, c, h):
        return u[d, (c // 3) % 2, c // 6, c % 3, h]

    def slink(d, c, h):
        return u[d, lax.rem(lax.div(c, 3), 2), lax.div(c, 6), lax.rem(c, 3), h]

    sub, lane = sublane(), lanes()
    low = sub < 4
    zrow = lax.rem(sub, 4)
    group = lax.div(lane, 16)
    xcol = lax.rem(lane, 16)

    for c in range(ROWS2):
        for pair in range(2):
            sft[c, pair] = jnp.where(low, link(2 * pair, c, 0), rs(link(2 * pair + 1, c, 0), 4))
            sbt[c, pair] = jnp.where(low, rs(link(2 * pair, c, 1), 4), link(2 * pair + 1, c, 1))
        for h in range(2):
            first, last = link(0, c, h), rs(link(0, c, h), -3)
            for k in range(1, 4):
                first = jnp.where(zrow == k, rs(link(k, c, h), k), first)
                last = jnp.where(zrow == k, rs(link(k, c, h), k - 3), last)
            sfz[c, h] = first
            sbz[c, h] = last
        first, last = link(0, c, 0), rl(link(0, c, 0), -112)
        for g in range(1, 8):
            first = jnp.where(group == g, rl(link(g % 4, c, g // 4), 16 * g), first)
            last = jnp.where(group == g, rl(link(g % 4, c, g // 4), 16 * (g - 7)), last)
        sfy[c] = first
        sby[c] = last

    def merged(items):
        out = items[0][1]
        for mask, value in items[1:]:
            out = jnp.where(mask, value, out)
        return out

    for w in range(2):
        six = range(6)
        sc[0, w] = merged([(sub == r, rs(link(0, w * 6 + r, 1), r - 4)) for r in six])
        sc[1, w] = merged([(group == g, rl(link(0, w * 6 + g, 1), 16 * g)) for g in six])
        sc[2, w] = merged([(sub == r, rs(link(1, w * 6 + r, 0), r - 3)) for r in six])
        sc[3, w] = merged(
            [
                ((group == g) & (zrow == t), rl(rs(link(1, t * 6 + g, w), t - 3), 16 * g))
                for t in range(2)
                for g in six
            ]
        )
        sc[4, w] = merged([(group == g, rl(link(2, w * 6 + g, 0), 16 * (g - 7))) for g in six])
        sc[5, w] = merged(
            [
                ((group == g) & (zrow == t), rl(rs(link(2, t * 6 + g, w), t), 16 * (g - 7)))
                for t in range(2)
                for g in six
            ]
        )

    def send(n, src, dst, target):
        return pltpu.make_async_remote_copy(
            src_ref=src,
            dst_ref=dst,
            send_sem=send_sem.at[n],
            recv_sem=recv_sem.at[n],
            device_id=target,
            device_id_type=MESH,
        )

    two = pl.ds(0, ROWS2)
    corner = [
        send(6 + n, sc.at[n], hc.at[n], at(((back, 1), (ahead, -1))))
        for n, (back, ahead) in enumerate(CORNERS)
    ]
    ahead_faces = [
        send(0, sft, hft.at[two], at(((0, -1),))),
        send(1, sfz, hfz.at[two], at(((1, -1),))),
        send(2, sfy, hfy.at[two], at(((2, -1),))),
    ]
    back_faces = [
        send(3, sbt, hbt.at[two], at(((0, 1),))),
        send(4, sbz, hbz.at[two], at(((1, 1),))),
        send(5, sby, hby.at[two], at(((2, 1),))),
    ]
    pl.semaphore_wait(barrier, len(targets))
    for copy in ahead_faces + back_faces + corner:
        copy.start()

    def ahead_x(field):
        return jnp.where(xcol == 15, rl(field, 15), rl(field, -1))

    def products(n, carry):
        pair, h = lax.div(n, 2), lax.rem(n, 2)
        mu = lax.div(pair, 3)
        nu = lax.rem(mu + 1 + lax.rem(pair, 3), 4)
        own = gather(lambda c: link(mu, c, h))
        far = gather(lambda c: v[pair, c, h])
        prod = mul_nn(own, far)

        def put_p(c, value):
            p[pair, c, h] = value

        def put_l(c, value):
            l[pair, c, h] = value

        scatter(put_p, prod)
        scatter(put_l, mul_hn(prod, gather(lambda c: link(nu, c, h))))
        return carry

    def shift_x(c, carry):
        for j in range(3):
            for h in range(2):
                v[9 + j, c, h] = ahead_x(slink(j, c, h))
        return carry

    lax.fori_loop(0, FULL, shift_x, 0)
    lax.fori_loop(18, 24, products, 0)

    for copy in ahead_faces:
        copy.wait_recv()

    def complete(ref, index):
        m = gather(lambda c: ref[(c,) + index], 2)

        def put(c, value):
            ref[(c,) + index] = value

        scatter(put, [third_row(m)], 2)

    for n in range(2):
        complete(hft, (n,))
        complete(hfz, (n,))
    complete(hfy, ())

    def shift_ahead(c, carry):
        for j in range(3):
            nu = 1 + j
            v0, v1 = slink(nu, c, 0), slink(nu, c, 1)
            r0, r1 = rs(v0, 4), rs(v1, 4)
            halo = hft[c, nu // 2]
            halo = halo if nu % 2 else rs(halo, 4)
            v[j, c, 0] = jnp.where(low, r0, r1)
            v[j, c, 1] = jnp.where(low, r1, halo)
        for j in range(3):
            nu = (2 + j) % 4
            for h in range(2):
                v[3 + j, c, h] = jnp.where(
                    zrow == 3, rs(hfz[c, h], 3 - nu), rs(slink(nu, c, h), -1)
                )
        halo = hfy[c]
        for j in range(3):
            nu = (3 + j) % 4
            for h in range(2):
                v[6 + j, c, h] = jnp.where(
                    group == 7, rl(halo, 16 * (7 - h * 4 - nu)), rl(slink(nu, c, h), -16)
                )
        return carry

    lax.fori_loop(0, FULL, shift_ahead, 0)
    lax.fori_loop(0, 18, products, 0)

    def plaquettes(n, carry):
        index, h = lax.div(n, 2), lax.rem(n, 2)
        far = lax.div(index, 4)
        mu = lax.rem(index, 4)
        nu = lax.rem(mu + 1 + far, 4)
        q = mul_nh(
            gather(lambda c: p[mu * 3 + far, c, h]), gather(lambda c: p[nu * 3 + 2 - far, c, h])
        )
        n = 0
        for i in range(3):
            a[index, n, h] = q[i][i][1] + q[i][i][1]
            n += 1
        for i in range(3):
            for j in range(i + 1, 3):
                a[index, n, h] = q[i][j][0] - q[j][i][0]
                a[index, n + 1, h] = q[i][j][1] + q[j][i][1]
                n += 2
        return carry

    lax.fori_loop(0, 12, plaquettes, 0)

    for copy in back_faces + corner:
        copy.wait_recv()
    for n in range(2):
        complete(hbt, (n,))
        complete(hbz, (n,))
    complete(hby, ())

    def face(ref, index, own, far12, out):
        far = gather(far12, 2)
        far = far + [third_row(far)]
        prod = mul_nn(gather(lambda c: ref[(c,) + index]), far)

        def put(c, value):
            out[(c,) + index] = value

        scatter(put, mul_hn(prod, gather(own)))

    def own_t(c):
        field = hbt[c, 0]
        return jnp.where(low, field, rs(field, 4))

    def far_t0(c):
        return jnp.where(sub == 7, rs(hc[0, c // 6], 7 - c % 6), rs(hbt[c, 0], 3))

    def far_t1(c):
        field = hbt[c, 0]
        edge = rl(rs(hc[1, c // 6], 4), 16 * (7 - c % 6))
        return jnp.where(
            low, jnp.where(group == 7, edge, rl(field, -16)), ahead_x(rs(field, 4))
        )

    face(hbt, (0,), own_t, far_t0, lt)
    face(hbt, (1,), own_t, far_t1, lt)

    for h in range(2):

        def own_z(c):
            field = hbz[c, h]
            return jnp.where(
                zrow == 0,
                rs(field, -1),
                jnp.where(zrow == 2, rs(field, 1), jnp.where(zrow == 3, rs(field, 2), field)),
            )

        def far_z(c):
            if h == 0:
                step_t = jnp.where(low, rs(hbz[c, 0], 3), rs(hbz[c, 1], 3))
            else:
                step_t = jnp.where(low, rs(hbz[c, 1], 3), rs(hc[2, c // 6], 4 - c % 6))
            field = hbz[c, h]
            edge = rl(rs(hc[3, h], 2 - c // 6), 16 * (7 - c % 6))
            step_y = jnp.where(group == 7, edge, rl(rs(field, 1), -16))
            step_x = ahead_x(rs(field, 2))
            return jnp.where(zrow == 0, step_t, jnp.where(zrow == 3, step_x, step_y))

        face(hbz, (h,), own_z, far_z, lz)

    def own_y(c):
        field = hby[c]
        slot = lax.rem(group, 4)
        return jnp.where(
            slot == 0,
            rl(field, -32),
            jnp.where(slot == 1, rl(field, -16), jnp.where(slot == 3, rl(field, 16), field)),
        )

    def far_y(c):
        field = hby[c]
        slot = lax.rem(group, 4)
        turned = rs(field, 4)
        edge = rs(rl(hc[4, c // 6], 16 * (4 - c % 6)), 4)
        high = jnp.where(group == 4, edge, rl(turned, 32))
        step_t = jnp.where(low, rl(turned, -32), high)
        edge0 = rs(rl(hc[5, 0], 16 * (1 - c % 6)), 3 - c // 6)
        edge1 = rs(rl(hc[5, 1], 16 * (5 - c % 6)), 3 - c // 6)
        step_z = jnp.where(
            zrow == 3, jnp.where(group == 1, edge0, edge1), rl(rs(field, -1), -16)
        )
        step_x = rl(ahead_x(field), 16)
        return jnp.where(slot == 0, step_t, jnp.where(slot == 3, step_x, step_z))

    face(hby, (), own_y, far_y, ly)

    def shift_back(c, carry):
        for h in range(2):
            for mu in range(4):
                terms = []
                for j in range(3):
                    nu = (mu + 1 + j) % 4
                    field = l[mu * 3 + j, c, h]
                    if nu == 0:
                        turned = rs(l[mu * 3 + j, c, 0], 4)
                        if h == 0:
                            halo = lt[c, mu // 2]
                            moved = jnp.where(low, rs(halo, 4) if mu % 2 else halo, turned)
                        else:
                            moved = jnp.where(low, turned, rs(field, 4))
                    elif nu == 1:
                        moved = jnp.where(zrow == 0, rs(lz[c, h], -mu), rs(field, 1))
                    elif nu == 2:
                        moved = jnp.where(
                            group == 0, rl(ly[c], -16 * (h * 4 + mu)), rl(field, 16)
                        )
                    else:
                        moved = jnp.where(xcol == 0, rl(field, -15), rl(field, 1))
                    terms.append(moved)
                s[mu, c, h] = total(terms)
        return carry

    lax.fori_loop(0, FULL, shift_back, 0)

    def forces(n, carry):
        mu, h = lax.div(n, 2), lax.rem(n, 2)
        w = mul_nn(gather(lambda c: link(mu, c, h)), gather(lambda c: s[mu, c, h]))
        prev = lax.rem(mu + 3, 4)
        pick = 4 + lax.rem(mu, 2)
        sign = 1.0 - 2.0 * lax.div(mu, 2).astype(jnp.float32)

        def extra(k):
            return a[mu, k, h] - a[prev, k, h] + sign * a[pick, k, h]

        diag = [w[i][i][1] + w[i][i][1] + extra(i) for i in range(3)]
        third = total(diag) * (1.0 / 3.0)
        for i in range(3):
            o[mu, 0, i, i, h] = jnp.zeros((8, 128), jnp.float32)
            o[mu, 1, i, i, h] = (0.5 * COEFF) * (diag[i] - third)
        k = 3
        for i in range(3):
            for j in range(i + 1, 3):
                re = (0.5 * COEFF) * (w[i][j][0] - w[j][i][0] + extra(k))
                im = (0.5 * COEFF) * (w[i][j][1] + w[j][i][1] + extra(k + 1))
                o[mu, 0, i, j, h] = re
                o[mu, 0, j, i, h] = -re
                o[mu, 1, i, j, h] = im
                o[mu, 1, j, i, h] = im
                k += 2
        return carry

    stores = [pltpu.make_async_copy(o.at[d], o_hbm.at[d], out_sem.at[d]) for d in range(4)]
    for d in range(4):
        lax.fori_loop(2 * d, 2 * d + 2, forces, 0)
        stores[d].start()
    for copy in ahead_faces + back_faces + corner:
        copy.wait_send()
    for store in stores:
        store.wait()


def per_device(links):
    shape = (4, 2, 3, 3, 2, 8, 128)
    f32 = jnp.float32
    out = pl.pallas_call(
        kernel,
        out_shape=jax.ShapeDtypeStruct(shape, f32),
        in_specs=[pl.BlockSpec(memory_space=pltpu.HBM)],
        out_specs=pl.BlockSpec(memory_space=pltpu.HBM),
        scratch_shapes=[
            pltpu.VMEM(shape, f32),
            pltpu.VMEM((12, FULL, 2, 8, 128), f32),
            pltpu.VMEM((12, FULL, 2, 8, 128), f32),
            pltpu.VMEM((12, FULL, 2, 8, 128), f32),
            pltpu.VMEM((4, FULL, 2, 8, 128), f32),
            pltpu.VMEM((6, 9, 2, 8, 128), f32),
            pltpu.VMEM(shape, f32),
        ]
        + [pltpu.VMEM((ROWS2, 2, 8, 128), f32)] * 4
        + [pltpu.VMEM((ROWS2, 8, 128), f32)] * 2
        + [pltpu.VMEM((6, 2, 8, 128), f32)]
        + [pltpu.VMEM((FULL, 2, 8, 128), f32)] * 4
        + [pltpu.VMEM((FULL, 8, 128), f32)] * 2
        + [pltpu.VMEM((6, 2, 8, 128), f32)]
        + [pltpu.VMEM((FULL, 2, 8, 128), f32)] * 2
        + [pltpu.VMEM((FULL, 8, 128), f32)]
        + [
            pltpu.SemaphoreType.DMA((4,)),
            pltpu.SemaphoreType.DMA((4,)),
            pltpu.SemaphoreType.DMA((12,)),
            pltpu.SemaphoreType.DMA((12,)),
        ],
        compiler_params=pltpu.CompilerParams(collective_id=0, has_side_effects=True),
        name="force",
    )(links.reshape(shape))
    return out.reshape(links.shape)


def solution(mesh):
    return jax.shard_map(
        per_device,
        mesh=mesh,
        in_specs=(P(None, None, None, None, "ta", "gz", "gx"),),
        out_specs=P(None, None, None, None, "ta", "gz", "gx"),
        check_vma=False,
    )
```

time: 70.4 us -> 22.4 us (0.32)
  the two profiles are of different devices: /device:TPU:14 before, /device:TPU:6 now
where the time goes in v1:
time: 22.4 us; the launch traced here: 22.3 us
  Pallas kernels  20.4 us (91%)
  local copies, waits for them, and re-layouts  1.92 us (9%)
    pallas_call x1, Pallas kernels, per_device(): pl.pallas_call(kernel, out_shape=jax.ShapeDtypeStruct(shape, f32), in_spe...  20.4 us
    unnamed x1, local copies, waits for them, and re-layouts  1.92 us

profile of v1, /device:TPU:6, one launch (start us, length us, event | category | flops | bytes accessed | tf_op | source)
XLA Modules:
  0.0 22.3 jit_solution(5131824703829925645)
XLA Ops:
  0.0 20.4 %force.1 = f32[4,2,3,3,2,8,128]{6,5,4,3,2,1,0:T(8,128)} custom-call(f32[4,2,3,3,2,8,128]{6,5,4,3,2,1,0:T(8,128)} %bitcast.3), custom_call_target="tpu_custom_call" | custom-call | tf_op jit(solution)/shard_map/force/pallas_call | solution.py:472
  20.4 1.9 %copy.3 = f32[4,2,3,3,4,4,128]{6,5,4,3,2,1,0:T(4,128)} copy(f32[4,2,3,3,4,4,128]{6,5,4,3,2,1,0:T(4,128)} %bitcast.2) | data formatting | bytes 1179648

commit v2 on v1

v2 whole, which is shorter than its diff:
```python
import jax
import jax.numpy as jnp
from jax import lax
from jax.experimental import pallas as pl
from jax.experimental.pallas import tpu as pltpu
from jax.sharding import PartitionSpec as P

COEFF = -1.9
MESH = pl.DeviceIdType.MESH
AXES = ("ta", "gz", "gx")
ROWS2 = 12
FULL = 18
CORNERS = ((0, 1), (0, 2), (1, 0), (1, 2), (2, 0), (2, 1))


def rs(v, k):
    k = k % 8
    return v if k == 0 else pltpu.roll(v, k, axis=0)


def rl(v, k):
    k = k % 128
    return v if k == 0 else pltpu.roll(v, k, axis=1)


def sublane():
    return lax.broadcasted_iota(jnp.int32, (8, 128), 0)


def lanes():
    return lax.broadcasted_iota(jnp.int32, (8, 128), 1)


def total(terms):
    out = terms[0]
    for t in terms[1:]:
        out = out + t
    return out


def mul_nn(a, b):
    return [
        [
            (
                total([a[i][k][0] * b[k][j][0] for k in range(3)])
                - total([a[i][k][1] * b[k][j][1] for k in range(3)]),
                total([a[i][k][0] * b[k][j][1] for k in range(3)])
                + total([a[i][k][1] * b[k][j][0] for k in range(3)]),
            )
            for j in range(3)
        ]
        for i in range(3)
    ]


def mul_hn(a, b):
    return [
        [
            (
                total([a[k][i][0] * b[k][j][0] for k in range(3)])
                + total([a[k][i][1] * b[k][j][1] for k in range(3)]),
                total([a[k][i][0] * b[k][j][1] for k in range(3)])
                - total([a[k][i][1] * b[k][j][0] for k in range(3)]),
            )
            for j in range(3)
        ]
        for i in range(3)
    ]


def mul_nh(a, b):
    return [
        [
            (
                total([a[i][k][0] * b[j][k][0] for k in range(3)])
                + total([a[i][k][1] * b[j][k][1] for k in range(3)]),
                total([a[i][k][1] * b[j][k][0] for k in range(3)])
                - total([a[i][k][0] * b[j][k][1] for k in range(3)]),
            )
            for j in range(3)
        ]
        for i in range(3)
    ]


def third_row(m):
    row = []
    for col in range(3):
        n, q = (col + 1) % 3, (col + 2) % 3
        r0n, i0n = m[0][n]
        r0q, i0q = m[0][q]
        r1n, i1n = m[1][n]
        r1q, i1q = m[1][q]
        row.append(
            (
                (r0n * r1q - i0n * i1q) - (r0q * r1n - i0q * i1n),
                (r0q * i1n + i0q * r1n) - (r0n * i1q + i0n * r1q),
            )
        )
    return row


def anti(w):
    nine = [w[i][i][1] + w[i][i][1] for i in range(3)]
    for i in range(3):
        for j in range(i + 1, 3):
            nine += [w[i][j][0] - w[j][i][0], w[i][j][1] + w[j][i][1]]
    return nine


def gather(entry, rows=3):
    return [[(entry(i * 6 + j), entry(i * 6 + 3 + j)) for j in range(3)] for i in range(rows)]


def scatter(put, m, first=0):
    for i, row in enumerate(m):
        for j, (re, im) in enumerate(row):
            put((first + i) * 6 + j, re)
            put((first + i) * 6 + 3 + j, im)


def kernel(
    x_hbm, o, u, v, p, l, a,
    sf, sb, sc, hf, hb, hc, far, near, lh,
    in_sem, send_sem, recv_sem,
):
    me = {axis: lax.axis_index(axis) for axis in AXES}
    size = {axis: lax.axis_size(axis) for axis in AXES}
    beside = {
        (d, step): lax.rem(me[AXES[d]] + (step + size[AXES[d]]), size[AXES[d]])
        for d in range(3)
        for step in (-1, 1)
    }

    def at(*steps):
        return {AXES[d]: beside[d, step] for d, step in steps}

    barrier = pltpu.get_barrier_semaphore()
    targets = [at((d, step)) for d in range(3) for step in (-1, 1)]
    targets += [at((back, 1), (ahead, -1)) for back, ahead in CORNERS]
    for target in targets:
        pl.semaphore_signal(barrier, inc=1, device_id=target, device_id_type=MESH)

    loads = [pltpu.make_async_copy(x_hbm.at[d], u.at[d], in_sem.at[d]) for d in range(4)]
    for load in loads:
        load.start()
    for load in loads:
        load.wait()

    def link(d, c, h):
        return u[d, (c // 3) % 2, c // 6, c % 3, h]

    sub, lane = sublane(), lanes()
    low = sub < 4
    zrow = lax.rem(sub, 4)
    group = lax.div(lane, 16)
    slot = lax.rem(group, 4)
    xcol = lax.rem(lane, 16)

    for c in range(ROWS2):
        for pair in range(2):
            sf[pair, c] = jnp.where(low, link(2 * pair, c, 0), rs(link(2 * pair + 1, c, 0), 4))
            sb[pair, c] = jnp.where(low, rs(link(2 * pair, c, 1), 4), link(2 * pair + 1, c, 1))
        for h in range(2):
            first, last = link(0, c, h), rs(link(0, c, h), -3)
            for k in range(1, 4):
                first = jnp.where(zrow == k, rs(link(k, c, h), k), first)
                last = jnp.where(zrow == k, rs(link(k, c, h), k - 3), last)
            sf[2 + h, c] = first
            sb[2 + h, c] = last
        first, last = link(0, c, 0), rl(link(0, c, 0), -112)
        for g in range(1, 8):
            first = jnp.where(group == g, rl(link(g % 4, c, g // 4), 16 * g), first)
            last = jnp.where(group == g, rl(link(g % 4, c, g // 4), 16 * (g - 7)), last)
        sf[4, c] = first
        sb[4, c] = last

    def merged(items):
        out = items[0][1]
        for mask, value in items[1:]:
            out = jnp.where(mask, value, out)
        return out

    for w in range(2):
        six = range(6)
        sc[0, w] = merged([(sub == r, rs(link(0, w * 6 + r, 1), r - 4)) for r in six])
        sc[1, w] = merged([(group == g, rl(link(0, w * 6 + g, 1), 16 * g)) for g in six])
        sc[2, w] = merged([(sub == r, rs(link(1, w * 6 + r, 0), r - 3)) for r in six])
        sc[3, w] = merged(
            [
                ((group == g) & (zrow == t), rl(rs(link(1, t * 6 + g, w), t - 3), 16 * g))
                for t in range(2)
                for g in six
            ]
        )
        sc[4, w] = merged([(group == g, rl(link(2, w * 6 + g, 0), 16 * (g - 7))) for g in six])
        sc[5, w] = merged(
            [
                ((group == g) & (zrow == t), rl(rs(link(2, t * 6 + g, w), t), 16 * (g - 7)))
                for t in range(2)
                for g in six
            ]
        )

    def send(n, src, dst, target):
        return pltpu.make_async_remote_copy(
            src_ref=src,
            dst_ref=dst,
            send_sem=send_sem.at[n],
            recv_sem=recv_sem.at[n],
            device_id=target,
            device_id_type=MESH,
        )

    corner = [
        send(6 + n, sc.at[n], hc.at[n], at((back, 1), (ahead, -1)))
        for n, (back, ahead) in enumerate(CORNERS)
    ]
    tiles = (pl.ds(0, 2), pl.ds(2, 2), pl.ds(4, 1))
    two = pl.ds(0, ROWS2)
    ahead_faces = [
        send(d, sf.at[tiles[d]], hf.at[tiles[d], two], at((d, -1))) for d in range(3)
    ]
    back_faces = [
        send(3 + d, sb.at[tiles[d]], hb.at[tiles[d], two], at((d, 1))) for d in range(3)
    ]
    pl.semaphore_wait(barrier, len(targets))
    for copy in corner:
        copy.start()
    for d in (1, 0, 2):
        ahead_faces[d].start()
        back_faces[d].start()

    def ahead_x(field):
        return jnp.where(xcol == 15, rl(field, 15), rl(field, -1))

    def products(n, carry):
        pair, h = lax.div(n, 2), lax.rem(n, 2)
        mu = lax.div(pair, 3)
        nu = lax.rem(mu + 1 + lax.rem(pair, 3), 4)
        prod = mul_nn(gather(lambda c: link(mu, c, h)), gather(lambda c: v[pair, c, h]))

        def put_p(c, value):
            p[pair, c, h] = value

        def put_l(c, value):
            l[pair, c, h] = value

        scatter(put_p, prod)
        scatter(put_l, mul_hn(prod, gather(lambda c: link(nu, c, h))))
        return carry

    def plaquettes(n, carry):
        index, h = lax.div(n, 2), lax.rem(n, 2)
        step, mu = lax.div(index, 4), lax.rem(index, 4)
        nu = lax.rem(mu + 1 + step, 4)
        q = mul_nh(
            gather(lambda c: p[mu * 3 + step, c, h]), gather(lambda c: p[nu * 3 + 2 - step, c, h])
        )
        for n, value in enumerate(anti(q)):
            a[index, n, h] = value
        return carry

    def complete(ref, k):
        m = gather(lambda c: ref[k, c], 2)

        def put(c, value):
            ref[k, c] = value

        scatter(put, [third_row(m)], 2)

    def move_x(mu):
        pair = mu * 3 + 2 - mu
        for c in range(FULL):
            for h in range(2):
                field = l[pair, c, h]
                v[pair, c, h] = jnp.where(xcol == 0, rl(field, -15), rl(field, 1))

    for c in range(FULL):
        for j in range(3):
            v[j, c, 0] = jnp.where(low, rs(link(1 + j, c, 0), 4), rs(link(1 + j, c, 1), 4))
            for h in range(2):
                v[9 + j, c, h] = ahead_x(link(j, c, h))
    lax.fori_loop(18, 24, products, 0)
    lax.fori_loop(0, 3, lambda j, carry: products(2 * j, carry), 0)

    ahead_faces[2].wait_recv()
    complete(hf, 4)
    for c in range(FULL):
        for j in range(3):
            for h in range(2):
                nu = (3 + j) % 4
                v[6 + j, c, h] = jnp.where(
                    group == 7, rl(hf[4, c], 16 * (7 - h * 4 - nu)), rl(link(nu, c, h), -16)
                )
    lax.fori_loop(12, 18, products, 0)

    ahead_faces[0].wait_recv()
    for k in range(2):
        complete(hf, k)
    for c in range(FULL):
        for j in range(3):
            nu = 1 + j
            halo = hf[nu // 2, c]
            v[j, c, 1] = jnp.where(
                low, rs(link(nu, c, 1), 4), halo if nu % 2 else rs(halo, 4)
            )
    lax.fori_loop(0, 3, lambda j, carry: products(2 * j + 1, carry), 0)
    move_x(0)
    move_x(2)
    lax.fori_loop(4, 10, plaquettes, 0)

    ahead_faces[1].wait_recv()
    for k in range(2, 4):
        complete(hf, k)
    for c in range(FULL):
        for j in range(3):
            for h in range(2):
                nu = (2 + j) % 4
                v[3 + j, c, h] = jnp.where(
                    zrow == 3, rs(hf[2 + h, c], 3 - nu), rs(link(nu, c, h), -1)
                )
    lax.fori_loop(6, 12, products, 0)
    move_x(1)
    lax.fori_loop(0, 4, plaquettes, 0)
    lax.fori_loop(10, 12, plaquettes, 0)

    for copy in back_faces + corner:
        copy.wait_recv()
    for k in range(5):
        complete(hb, k)

    def step_t0(c):
        return jnp.where(sub == 7, rs(hc[0, c // 6], 7 - c % 6), rs(hb[0, c], 3))

    def step_t1(c):
        field = hb[0, c]
        edge = rl(rs(hc[1, c // 6], 4), 16 * (7 - c % 6))
        return jnp.where(
            low, jnp.where(group == 7, edge, rl(field, -16)), ahead_x(rs(field, 4))
        )

    def step_z(h):
        def step(c):
            field = hb[2 + h, c]
            if h == 0:
                along_t = jnp.where(low, rs(field, 3), rs(hb[3, c], 3))
            else:
                along_t = jnp.where(low, rs(field, 3), rs(hc[2, c // 6], 4 - c % 6))
            edge = rl(rs(hc[3, h], 2 - c // 6), 16 * (7 - c % 6))
            along_y = jnp.where(group == 7, edge, rl(rs(field, 1), -16))
            along_x = ahead_x(rs(field, 2))
            return jnp.where(zrow == 0, along_t, jnp.where(zrow == 3, along_x, along_y))

        return step

    def step_y(c):
        field = hb[4, c]
        turned = rs(field, 4)
        edge = rs(rl(hc[4, c // 6], 16 * (4 - c % 6)), 4)
        high = jnp.where(group == 4, edge, rl(turned, 32))
        along_t = jnp.where(low, rl(turned, -32), high)
        edge0 = rs(rl(hc[5, 0], 16 * (1 - c % 6)), 3 - c // 6)
        edge1 = rs(rl(hc[5, 1], 16 * (5 - c % 6)), 3 - c // 6)
        along_z = jnp.where(
            zrow == 3, jnp.where(group == 1, edge0, edge1), rl(rs(field, -1), -16)
        )
        along_x = rl(ahead_x(field), 16)
        return jnp.where(slot == 0, along_t, jnp.where(slot == 3, along_x, along_z))

    for k, step in enumerate((step_t0, step_t1, step_z(0), step_z(1), step_y)):
        m = gather(step, 2)

        def put_far(c, value):
            far[k, c] = value

        scatter(put_far, m + [third_row(m)])
    for c in range(FULL):
        field = hb[0, c]
        near[0, c] = jnp.where(low, field, rs(field, 4))
        near[1, c] = jnp.where(low, field, rs(field, 4))
        for h in range(2):
            field = hb[2 + h, c]
            near[2 + h, c] = jnp.where(
                zrow == 0,
                rs(field, -1),
                jnp.where(zrow == 2, rs(field, 1), jnp.where(zrow == 3, rs(field, 2), field)),
            )
        field = hb[4, c]
        near[4, c] = jnp.where(
            slot == 0,
            rl(field, -32),
            jnp.where(slot == 1, rl(field, -16), jnp.where(slot == 3, rl(field, 16), field)),
        )

    def faces(k, carry):
        prod = mul_nn(gather(lambda c: hb[k, c]), gather(lambda c: far[k, c]))

        def put(c, value):
            lh[k, c] = value

        scatter(put, mul_hn(prod, gather(lambda c: near[k, c])))
        return carry

    lax.fori_loop(0, 5, faces, 0)

    for c in range(FULL):
        for mu in range(4):
            if mu != 0:
                pair = mu * 3 + 3 - mu
                halo = lh[mu // 2, c]
                turned = rs(l[pair, c, 0], 4)
                v[pair, c, 0] = jnp.where(low, rs(halo, 4) if mu % 2 else halo, turned)
                v[pair, c, 1] = jnp.where(low, turned, rs(l[pair, c, 1], 4))
            for h in range(2):
                if mu != 1:
                    pair = mu * 3 + (0 - mu) % 4
                    v[pair, c, h] = jnp.where(
                        zrow == 0, rs(lh[2 + h, c], -mu), rs(l[pair, c, h], 1)
                    )
                if mu != 2:
                    pair = mu * 3 + (1 - mu) % 4
                    v[pair, c, h] = jnp.where(
                        group == 0, rl(lh[4, c], -16 * (h * 4 + mu)), rl(l[pair, c, h], 16)
                    )

    def forces(n, carry):
        mu, h = lax.div(n, 2), lax.rem(n, 2)
        staple = gather(
            lambda c: v[mu * 3, c, h] + v[mu * 3 + 1, c, h] + v[mu * 3 + 2, c, h]
        )
        w = anti(mul_nn(gather(lambda c: link(mu, c, h)), staple))
        prev = lax.rem(mu + 3, 4)
        pick = 4 + lax.rem(mu, 2)
        sign = 1.0 - 2.0 * lax.div(mu, 2).astype(jnp.float32)
        nine = [
            w[k] + (a[mu, k, h] - a[prev, k, h] + sign * a[pick, k, h]) for k in range(9)
        ]
        third = (nine[0] + nine[1] + nine[2]) * (1.0 / 3.0)
        k = 3
        for i in range(3):
            o[mu, 0, i, i, h] = jnp.zeros((8, 128), jnp.float32)
            o[mu, 1, i, i, h] = (0.5 * COEFF) * (nine[i] - third)
            for j in range(i + 1, 3):
                re, im = (0.5 * COEFF) * nine[k], (0.5 * COEFF) * nine[k + 1]
                o[mu, 0, i, j, h] = re
                o[mu, 0, j, i, h] = -re
                o[mu, 1, i, j, h] = im
                o[mu, 1, j, i, h] = im
                k += 2
        return carry

    lax.fori_loop(0, 8, forces, 0)
    for copy in ahead_faces + back_faces + corner:
        copy.wait_send()


def per_device(links):
    shape = (4, 2, 3, 3, 2, 8, 128)

    def vmem(*lead):
        return pltpu.VMEM(lead + (8, 128), jnp.float32)

    pairs = vmem(12, FULL, 2)
    out = pl.pallas_call(
        kernel,
        out_shape=jax.ShapeDtypeStruct(shape, jnp.float32),
        in_specs=[pl.BlockSpec(memory_space=pltpu.HBM)],
        out_specs=pl.BlockSpec(memory_space=pltpu.VMEM),
        scratch_shapes=[
            vmem(4, 2, 3, 3, 2),
            pairs,
            pairs,
            pairs,
            vmem(6, 9, 2),
            vmem(5, ROWS2),
            vmem(5, ROWS2),
            vmem(6, 2),
            vmem(5, FULL),
            vmem(5, FULL),
            vmem(6, 2),
            vmem(5, FULL),
            vmem(5, FULL),
            vmem(5, FULL),
            pltpu.SemaphoreType.DMA((4,)),
            pltpu.SemaphoreType.DMA((12,)),
            pltpu.SemaphoreType.DMA((12,)),
        ],
        compiler_params=pltpu.CompilerParams(
            collective_id=0, has_side_effects=True, vmem_limit_bytes=16 * 1024 * 1024
        ),
        name="force",
    )(pltpu.with_memory_space_constraint(links.reshape(shape), pltpu.HBM))
    return out.reshape(links.shape)


def solution(mesh):
    return jax.shard_map(
        per_device,
        mesh=mesh,
        in_specs=(P(None, None, None, None, "ta", "gz", "gx"),),
        out_specs=P(None, None, None, None, "ta", "gz", "gx"),
        check_vma=False,
    )
```

time: 22.4 us -> 19.4 us (0.87)
  the two profiles are of different devices: /device:TPU:6 before, /device:TPU:1 now
where the time goes in v2:
time: 19.4 us; the launch traced here: 19.3 us
  Pallas kernels  18.5 us (95%)
  local copies, waits for them, and re-layouts  0.82 us (4%)
    pallas_call x1, Pallas kernels, per_device(): pl.pallas_call(kernel, out_shape=jax.ShapeDtypeStruct(shape, jnp.float32)...  18.5 us
    unnamed x1, local copies, waits for them, and re-layouts  0.82 us

profile of v2, /device:TPU:1, one launch (start us, length us, event | category | flops | bytes accessed | tf_op | source)
XLA Modules:
  0.0 19.3 jit_solution(8877728095662573477)
XLA Ops:
  0.0 18.5 %force.1 = f32[4,2,3,3,2,8,128]{6,5,4,3,2,1,0:T(8,128)S(1)} custom-call(f32[4,2,3,3,2,8,128]{6,5,4,3,2,1,0:T(8,128)} %bitcast.3), custom_call_target="tpu_custom_call" | custom-call | tf_op jit(solution)/shard_map/force/pallas_call | solution.py:465
  18.5 0.8 %copy.3 = f32[4,2,3,3,4,4,128]{6,5,4,3,2,1,0:T(4,128)} copy(f32[4,2,3,3,4,4,128]{6,5,4,3,2,1,0:T(4,128)S(1)} %bitcast.2) | data formatting | bytes 1179648

commit v3 on v2

--- a/solution.py
+++ b/solution.py
@@ -121,8 +121,8 @@
 
 def kernel(
     x_hbm, o, u, v, p, l, a,
-    sf, sb, sc, hf, hb, hc, far, near, lh,
-    in_sem, send_sem, recv_sem,
+    sf, sb, sc, hf, hb, hc, far, near, lh, staple, below, upper,
+    in_sem, send_sem, recv_sem, ready,
 ):
     me = {axis: lax.axis_index(axis) for axis in AXES}
     size = {axis: lax.axis_size(axis) for axis in AXES}
@@ -137,7 +137,6 @@
 
     barrier = pltpu.get_barrier_semaphore()
     targets = [at((d, step)) for d in range(3) for step in (-1, 1)]
-    targets += [at((back, 1), (ahead, -1)) for back, ahead in CORNERS]
     for target in targets:
         pl.semaphore_signal(barrier, inc=1, device_id=target, device_id_type=MESH)
 
@@ -225,11 +224,16 @@
         send(3 + d, sb.at[tiles[d]], hb.at[tiles[d], two], at((d, 1))) for d in range(3)
     ]
     pl.semaphore_wait(barrier, len(targets))
-    for copy in corner:
-        copy.start()
+    words = ((0, -1), (0, 1), (2, -1), (2, 1))
+    for n, word in enumerate(words):
+        pl.semaphore_signal(ready.at[n], inc=1, device_id=at(word), device_id_type=MESH)
     for d in (1, 0, 2):
+        back_faces[d].start()
         ahead_faces[d].start()
-        back_faces[d].start()
+    for n, through in enumerate(((0,), (2,), (4, 5), (1, 3))):
+        pl.semaphore_wait(ready.at[n], 1)
+        for m in through:
+            corner[m].start()
 
     def ahead_x(field):
         return jnp.where(xcol == 15, rl(field, 15), rl(field, -1))
@@ -324,11 +328,6 @@
     move_x(1)
     lax.fori_loop(0, 4, plaquettes, 0)
     lax.fori_loop(10, 12, plaquettes, 0)
-
-    for copy in back_faces + corner:
-        copy.wait_recv()
-    for k in range(5):
-        complete(hb, k)
 
     def step_t0(c):
         return jnp.where(sub == 7, rs(hc[0, c // 6], 7 - c % 6), rs(hb[0, c], 3))
@@ -368,31 +367,6 @@
         along_x = rl(ahead_x(field), 16)
         return jnp.where(slot == 0, along_t, jnp.where(slot == 3, along_x, along_z))
 
-    for k, step in enumerate((step_t0, step_t1, step_z(0), step_z(1), step_y)):
-        m = gather(step, 2)
-
-        def put_far(c, value):
-            far[k, c] = value
-
-        scatter(put_far, m + [third_row(m)])
-    for c in range(FULL):
-        field = hb[0, c]
-        near[0, c] = jnp.where(low, field, rs(field, 4))
-        near[1, c] = jnp.where(low, field, rs(field, 4))
-        for h in range(2):
-            field = hb[2 + h, c]
-            near[2 + h, c] = jnp.where(
-                zrow == 0,
-                rs(field, -1),
-                jnp.where(zrow == 2, rs(field, 1), jnp.where(zrow == 3, rs(field, 2), field)),
-            )
-        field = hb[4, c]
-        near[4, c] = jnp.where(
-            slot == 0,
-            rl(field, -32),
-            jnp.where(slot == 1, rl(field, -16), jnp.where(slot == 3, rl(field, 16), field)),
-        )
-
     def faces(k, carry):
         prod = mul_nn(gather(lambda c: hb[k, c]), gather(lambda c: far[k, c]))
 
@@ -402,40 +376,26 @@
         scatter(put, mul_hn(prod, gather(lambda c: near[k, c])))
         return carry
 
-    lax.fori_loop(0, 5, faces, 0)
-
-    for c in range(FULL):
-        for mu in range(4):
-            if mu != 0:
-                pair = mu * 3 + 3 - mu
-                halo = lh[mu // 2, c]
-                turned = rs(l[pair, c, 0], 4)
-                v[pair, c, 0] = jnp.where(low, rs(halo, 4) if mu % 2 else halo, turned)
-                v[pair, c, 1] = jnp.where(low, turned, rs(l[pair, c, 1], 4))
-            for h in range(2):
-                if mu != 1:
-                    pair = mu * 3 + (0 - mu) % 4
-                    v[pair, c, h] = jnp.where(
-                        zrow == 0, rs(lh[2 + h, c], -mu), rs(l[pair, c, h], 1)
-                    )
-                if mu != 2:
-                    pair = mu * 3 + (1 - mu) % 4
-                    v[pair, c, h] = jnp.where(
-                        group == 0, rl(lh[4, c], -16 * (h * 4 + mu)), rl(l[pair, c, h], 16)
-                    )
-
-    def forces(n, carry):
+    def put_far(k, step):
+        m = gather(step, 2)
+
+        def put(c, value):
+            far[k, c] = value
+
+        scatter(put, m + [third_row(m)])
+
+    def uppers(n, carry):
         mu, h = lax.div(n, 2), lax.rem(n, 2)
-        staple = gather(
-            lambda c: v[mu * 3, c, h] + v[mu * 3 + 1, c, h] + v[mu * 3 + 2, c, h]
-        )
-        w = anti(mul_nn(gather(lambda c: link(mu, c, h)), staple))
         prev = lax.rem(mu + 3, 4)
         pick = 4 + lax.rem(mu, 2)
         sign = 1.0 - 2.0 * lax.div(mu, 2).astype(jnp.float32)
-        nine = [
-            w[k] + (a[mu, k, h] - a[prev, k, h] + sign * a[pick, k, h]) for k in range(9)
-        ]
+        for k in range(9):
+            upper[mu, k, h] = a[mu, k, h] - a[prev, k, h] + sign * a[pick, k, h]
+        return carry
+
+    def forces(mu, h, entry):
+        w = anti(mul_nn(gather(lambda c: link(mu, c, h)), gather(entry)))
+        nine = [w[k] + upper[mu, k, h] for k in range(9)]
         third = (nine[0] + nine[1] + nine[2]) * (1.0 / 3.0)
         k = 3
         for i in range(3):
@@ -448,9 +408,86 @@
                 o[mu, 1, i, j, h] = im
                 o[mu, 1, j, i, h] = im
                 k += 2
+
+    lax.fori_loop(0, 8, uppers, 0)
+    for copy in (back_faces[0], back_faces[2], corner[0], corner[1], corner[4], corner[5]):
+        copy.wait_recv()
+    for k in (0, 1, 4):
+        complete(hb, k)
+    put_far(0, step_t0)
+    put_far(1, step_t1)
+    put_far(4, step_y)
+    for c in range(FULL):
+        field = hb[0, c]
+        both = jnp.where(low, field, rs(field, 4))
+        near[0, c] = both
+        near[1, c] = both
+        field = hb[4, c]
+        near[4, c] = jnp.where(
+            slot == 0,
+            rl(field, -32),
+            jnp.where(slot == 1, rl(field, -16), jnp.where(slot == 3, rl(field, 16), field)),
+        )
+    lax.fori_loop(0, 3, lambda k, carry: faces(k + lax.div(k, 2) * 2, carry), 0)
+    for c in range(FULL):
+        for mu in range(4):
+            for h in range(2):
+                terms = []
+                if mu != 3:
+                    terms.append(v[mu * 3 + 2 - mu, c, h])
+                if mu != 0:
+                    pair = mu * 3 + 3 - mu
+                    turned = rs(l[pair, c, 0], 4)
+                    if h == 0:
+                        halo = lh[mu // 2, c]
+                        moved = jnp.where(low, rs(halo, 4) if mu % 2 else halo, turned)
+                    else:
+                        moved = jnp.where(low, turned, rs(l[pair, c, 1], 4))
+                    terms.append(moved)
+                if mu != 2:
+                    pair = mu * 3 + (1 - mu) % 4
+                    moved = jnp.where(
+                        group == 0, rl(lh[4, c], -16 * (h * 4 + mu)), rl(l[pair, c, h], 16)
+                    )
+                    terms.append(moved)
+                staple[mu, c, h] = total(terms)
+
+    def forces_z(h, carry):
+        forces(1, h, lambda c: staple[1, c, h])
         return carry
 
-    lax.fori_loop(0, 8, forces, 0)
+    lax.fori_loop(0, 2, forces_z, 0)
+
+    for copy in (back_faces[1], corner[2], corner[3]):
+        copy.wait_recv()
+    for k in (2, 3):
+        complete(hb, k)
+    put_far(2, step_z(0))
+    put_far(3, step_z(1))
+    for c in range(FULL):
+        for h in range(2):
+            field = hb[2 + h, c]
+            near[2 + h, c] = jnp.where(
+                zrow == 0,
+                rs(field, -1),
+                jnp.where(zrow == 2, rs(field, 1), jnp.where(zrow == 3, rs(field, 2), field)),
+            )
+    lax.fori_loop(2, 4, faces, 0)
+    for c in range(FULL):
+        for h in range(2):
+            for mu in (0, 2, 3):
+                pair = mu * 3 + (0 - mu) % 4
+                below[mu, c, h] = jnp.where(
+                    zrow == 0, rs(lh[2 + h, c], -mu), rs(l[pair, c, h], 1)
+                )
+
+    def forces_rest(n, carry):
+        m, h = lax.div(n, 2), lax.rem(n, 2)
+        mu = m + lax.div(m + 1, 2)
+        forces(mu, h, lambda c: staple[mu, c, h] + below[mu, c, h])
+        return carry
+
+    lax.fori_loop(0, 6, forces_rest, 0)
     for copy in ahead_faces + back_faces + corner:
         copy.wait_send()
 
@@ -482,9 +519,13 @@
             vmem(5, FULL),
             vmem(5, FULL),
             vmem(5, FULL),
+            vmem(4, FULL, 2),
+            vmem(4, FULL, 2),
+            vmem(4, 9, 2),
             pltpu.SemaphoreType.DMA((4,)),
             pltpu.SemaphoreType.DMA((12,)),
             pltpu.SemaphoreType.DMA((12,)),
+            pltpu.SemaphoreType.REGULAR((4,)),
         ],
         compiler_params=pltpu.CompilerParams(
             collective_id=0, has_side_effects=True, vmem_limit_bytes=16 * 1024 * 1024

time: 19.4 us -> 18.7 us (0.964)
  Pallas kernels: 18.5 us -> 17.8 us
    pallas_call x1, Pallas kernels: 18.5 us -> 17.8 us  [per_device(): pl.pallas_call(kernel, out_shape=jax.ShapeDtypeStruct(shape, jnp.float32)...]
where the time goes in v3:
time: 18.7 us; the launch traced here: 18.6 us
  Pallas kernels  17.8 us (95%)
  local copies, waits for them, and re-layouts  0.82 us (4%)
    pallas_call x1, Pallas kernels, per_device(): pl.pallas_call(kernel, out_shape=jax.ShapeDtypeStruct(shape, jnp.float32)...  17.8 us
    unnamed x1, local copies, waits for them, and re-layouts  0.82 us

profile of v3, /device:TPU:1, one launch (start us, length us, event | category | flops | bytes accessed | tf_op | source)
XLA Modules:
  0.0 18.6 jit_solution(696739628739753556)
XLA Ops:
  0.0 17.8 %force.1 = f32[4,2,3,3,2,8,128]{6,5,4,3,2,1,0:T(8,128)S(1)} custom-call(f32[4,2,3,3,2,8,128]{6,5,4,3,2,1,0:T(8,128)} %bitcast.3), custom_call_target="tpu_custom_call" | custom-call | tf_op jit(solution)/shard_map/force/pallas_call | solution.py:502
  17.8 0.8 %copy.3 = f32[4,2,3,3,4,4,128]{6,5,4,3,2,1,0:T(4,128)} copy(f32[4,2,3,3,4,4,128]{6,5,4,3,2,1,0:T(4,128)S(1)} %bitcast.2) | data formatting | bytes 1179648

commit v4 on v3

--- a/solution.py
+++ b/solution.py
@@ -29,6 +29,10 @@
 
 def lanes():
     return lax.broadcasted_iota(jnp.int32, (8, 128), 1)
+
+
+def pick(v, index):
+    return jnp.take_along_axis(v, index, axis=1, mode="promise_in_bounds")
 
 
 def total(terms):
@@ -121,7 +125,7 @@
 
 def kernel(
     x_hbm, o, u, v, p, l, a,
-    sf, sb, sc, hf, hb, hc, far, near, lh, staple, below, upper,
+    sf, sb, sc, hf, hb, hc, far, near, lh, own, pf, lf, staple, below,
     in_sem, send_sem, recv_sem, ready,
 ):
     me = {axis: lax.axis_index(axis) for axis in AXES}
@@ -155,24 +159,38 @@
     group = lax.div(lane, 16)
     slot = lax.rem(group, 4)
     xcol = lax.rem(lane, 16)
-
-    for c in range(ROWS2):
+    row16 = lane - xcol
+    to_next = row16 + lax.rem(xcol + 1, 16)
+    to_last = row16 + lax.rem(xcol + 15, 16)
+    own_row = lax.div(lane, 64) * 64 + 32 + xcol
+    next_x = lax.rem(row16 + 112, 128) + lax.rem(xcol + 1, 16)
+    time_row = lax.rem(lane + jnp.where(low, 32, 96), 128)
+
+    for c in range(FULL):
         for pair in range(2):
-            sf[pair, c] = jnp.where(low, link(2 * pair, c, 0), rs(link(2 * pair + 1, c, 0), 4))
-            sb[pair, c] = jnp.where(low, rs(link(2 * pair, c, 1), 4), link(2 * pair + 1, c, 1))
+            even, odd = 2 * pair, 2 * pair + 1
+            sb[pair, c] = jnp.where(low, rs(link(even, c, 1), 4), link(odd, c, 1))
+            if c < ROWS2:
+                sf[pair, c] = jnp.where(low, link(even, c, 0), rs(link(odd, c, 0), 4))
         for h in range(2):
-            first, last = link(0, c, h), rs(link(0, c, h), -3)
+            last = rs(link(0, c, h), -3)
             for k in range(1, 4):
-                first = jnp.where(zrow == k, rs(link(k, c, h), k), first)
                 last = jnp.where(zrow == k, rs(link(k, c, h), k - 3), last)
-            sf[2 + h, c] = first
             sb[2 + h, c] = last
-        first, last = link(0, c, 0), rl(link(0, c, 0), -112)
+            if c < ROWS2:
+                first = link(0, c, h)
+                for k in range(1, 4):
+                    first = jnp.where(zrow == k, rs(link(k, c, h), k), first)
+                sf[2 + h, c] = first
+        last = rl(link(0, c, 0), -112)
         for g in range(1, 8):
-            first = jnp.where(group == g, rl(link(g % 4, c, g // 4), 16 * g), first)
             last = jnp.where(group == g, rl(link(g % 4, c, g // 4), 16 * (g - 7)), last)
-        sf[4, c] = first
         sb[4, c] = last
+        if c < ROWS2:
+            first = link(0, c, 0)
+            for g in range(1, 8):
+                first = jnp.where(group == g, rl(link(g % 4, c, g // 4), 16 * g), first)
+            sf[4, c] = first
 
     def merged(items):
         out = items[0][1]
@@ -221,7 +239,7 @@
         send(d, sf.at[tiles[d]], hf.at[tiles[d], two], at((d, -1))) for d in range(3)
     ]
     back_faces = [
-        send(3 + d, sb.at[tiles[d]], hb.at[tiles[d], two], at((d, 1))) for d in range(3)
+        send(3 + d, sb.at[tiles[d], two], hb.at[tiles[d], two], at((d, 1))) for d in range(3)
     ]
     pl.semaphore_wait(barrier, len(targets))
     words = ((0, -1), (0, 1), (2, -1), (2, 1))
@@ -236,7 +254,7 @@
             corner[m].start()
 
     def ahead_x(field):
-        return jnp.where(xcol == 15, rl(field, 15), rl(field, -1))
+        return pick(field, to_next)
 
     def products(n, carry):
         pair, h = lax.div(n, 2), lax.rem(n, 2)
@@ -273,31 +291,60 @@
 
         scatter(put, [third_row(m)], 2)
 
-    def move_x(mu):
-        pair = mu * 3 + 2 - mu
-        for c in range(FULL):
-            for h in range(2):
-                field = l[pair, c, h]
-                v[pair, c, h] = jnp.where(xcol == 0, rl(field, -15), rl(field, 1))
+    def last_products(k, carry):
+        prod = mul_nn(gather(lambda c: own[k, c]), gather(lambda c: hf[k, c]))
+
+        def put_p(c, value):
+            pf[k, c] = value
+
+        def put_l(c, value):
+            lf[k, c] = value
+
+        scatter(put_p, prod)
+        scatter(put_l, mul_hn(prod, gather(lambda c: sb[k, c])))
+        return carry
+
+    def spread_z(field):
+        return jnp.where(
+            zrow == 0,
+            rs(field, -1),
+            jnp.where(zrow == 2, rs(field, 1), jnp.where(zrow == 3, rs(field, 2), field)),
+        )
 
     for c in range(FULL):
         for j in range(3):
             v[j, c, 0] = jnp.where(low, rs(link(1 + j, c, 0), 4), rs(link(1 + j, c, 1), 4))
             for h in range(2):
+                v[3 + j, c, h] = rs(link((2 + j) % 4, c, h), -1)
+                v[6 + j, c, h] = rl(link((3 + j) % 4, c, h), -16)
                 v[9 + j, c, h] = ahead_x(link(j, c, h))
-    lax.fori_loop(18, 24, products, 0)
+        for h in range(2):
+            own[2 + h, c] = spread_z(sb[2 + h, c])
+        own[4, c] = pick(sb[4, c], own_row)
+    lax.fori_loop(6, 24, products, 0)
     lax.fori_loop(0, 3, lambda j, carry: products(2 * j, carry), 0)
+    for c in range(FULL):
+        v[2, c, 0] = pick(l[2, c, 0], to_last)
+        v[1, c, 0] = rl(l[1, c, 0], 16)
+        for h in range(2):
+            v[4, c, h] = pick(l[4, c, h], to_last)
+            v[6, c, h] = pick(l[6, c, h], to_last)
+            v[11, c, h] = rl(l[11, c, h], 16)
 
     ahead_faces[2].wait_recv()
     complete(hf, 4)
+    lax.fori_loop(4, 5, last_products, 0)
     for c in range(FULL):
         for j in range(3):
+            nu = (3 + j) % 4
             for h in range(2):
-                nu = (3 + j) % 4
-                v[6 + j, c, h] = jnp.where(
-                    group == 7, rl(hf[4, c], 16 * (7 - h * 4 - nu)), rl(link(nu, c, h), -16)
-                )
-    lax.fori_loop(12, 18, products, 0)
+                turn = 16 * (7 - h * 4 - nu)
+                p[6 + j, c, h] = jnp.where(group == 7, rl(pf[4, c], turn), p[6 + j, c, h])
+                if j == 0:
+                    moved = pick(lf[4, c], 16 * (h * 4 + nu) + lax.rem(xcol + 15, 16))
+                    v[6, c, h] = jnp.where(group == 7, moved, v[6, c, h])
+                else:
+                    l[6 + j, c, h] = jnp.where(group == 7, rl(lf[4, c], turn), l[6 + j, c, h])
 
     ahead_faces[0].wait_recv()
     for k in range(2):
@@ -310,22 +357,26 @@
                 low, rs(link(nu, c, 1), 4), halo if nu % 2 else rs(halo, 4)
             )
     lax.fori_loop(0, 3, lambda j, carry: products(2 * j + 1, carry), 0)
-    move_x(0)
-    move_x(2)
+    for c in range(FULL):
+        v[2, c, 1] = pick(l[2, c, 1], to_last)
+        v[1, c, 1] = rl(l[1, c, 1], 16)
     lax.fori_loop(4, 10, plaquettes, 0)
 
     ahead_faces[1].wait_recv()
     for k in range(2, 4):
         complete(hf, k)
+    lax.fori_loop(2, 4, last_products, 0)
     for c in range(FULL):
         for j in range(3):
+            nu = (2 + j) % 4
             for h in range(2):
-                nu = (2 + j) % 4
-                v[3 + j, c, h] = jnp.where(
-                    zrow == 3, rs(hf[2 + h, c], 3 - nu), rs(link(nu, c, h), -1)
-                )
-    lax.fori_loop(6, 12, products, 0)
-    move_x(1)
+                p[3 + j, c, h] = jnp.where(zrow == 3, rs(pf[2 + h, c], 3 - nu), p[3 + j, c, h])
+                if j == 1:
+                    v[4, c, h] = jnp.where(zrow == 3, pick(lf[2 + h, c], to_last), v[4, c, h])
+                else:
+                    l[3 + j, c, h] = jnp.where(
+                        zrow == 3, rs(lf[2 + h, c], 3 - nu), l[3 + j, c, h]
+                    )
     lax.fori_loop(0, 4, plaquettes, 0)
     lax.fori_loop(10, 12, plaquettes, 0)
 
@@ -357,14 +408,13 @@
         field = hb[4, c]
         turned = rs(field, 4)
         edge = rs(rl(hc[4, c // 6], 16 * (4 - c % 6)), 4)
-        high = jnp.where(group == 4, edge, rl(turned, 32))
-        along_t = jnp.where(low, rl(turned, -32), high)
+        along_t = jnp.where((group == 4) & (sub >= 4), edge, pick(turned, time_row))
         edge0 = rs(rl(hc[5, 0], 16 * (1 - c % 6)), 3 - c // 6)
         edge1 = rs(rl(hc[5, 1], 16 * (5 - c % 6)), 3 - c // 6)
         along_z = jnp.where(
             zrow == 3, jnp.where(group == 1, edge0, edge1), rl(rs(field, -1), -16)
         )
-        along_x = rl(ahead_x(field), 16)
+        along_x = pick(field, next_x)
         return jnp.where(slot == 0, along_t, jnp.where(slot == 3, along_x, along_z))
 
     def faces(k, carry):
@@ -384,18 +434,13 @@
 
         scatter(put, m + [third_row(m)])
 
-    def uppers(n, carry):
-        mu, h = lax.div(n, 2), lax.rem(n, 2)
-        prev = lax.rem(mu + 3, 4)
-        pick = 4 + lax.rem(mu, 2)
-        sign = 1.0 - 2.0 * lax.div(mu, 2).astype(jnp.float32)
-        for k in range(9):
-            upper[mu, k, h] = a[mu, k, h] - a[prev, k, h] + sign * a[pick, k, h]
-        return carry
-
     def forces(mu, h, entry):
         w = anti(mul_nn(gather(lambda c: link(mu, c, h)), gather(entry)))
-        nine = [w[k] + upper[mu, k, h] for k in range(9)]
+        prev, other = lax.rem(mu + 3, 4), 4 + lax.rem(mu, 2)
+        sign = 1.0 - 2.0 * lax.div(mu, 2).astype(jnp.float32)
+        nine = [
+            w[k] + (a[mu, k, h] - a[prev, k, h] + sign * a[other, k, h]) for k in range(9)
+        ]
         third = (nine[0] + nine[1] + nine[2]) * (1.0 / 3.0)
         k = 3
         for i in range(3):
@@ -409,7 +454,6 @@
                 o[mu, 1, j, i, h] = im
                 k += 2
 
-    lax.fori_loop(0, 8, uppers, 0)
     for copy in (back_faces[0], back_faces[2], corner[0], corner[1], corner[4], corner[5]):
         copy.wait_recv()
     for k in (0, 1, 4):
@@ -423,11 +467,7 @@
         near[0, c] = both
         near[1, c] = both
         field = hb[4, c]
-        near[4, c] = jnp.where(
-            slot == 0,
-            rl(field, -32),
-            jnp.where(slot == 1, rl(field, -16), jnp.where(slot == 3, rl(field, 16), field)),
-        )
+        near[4, c] = pick(field, own_row)
     lax.fori_loop(0, 3, lambda k, carry: faces(k + lax.div(k, 2) * 2, carry), 0)
     for c in range(FULL):
         for mu in range(4):
@@ -446,14 +486,13 @@
                     terms.append(moved)
                 if mu != 2:
                     pair = mu * 3 + (1 - mu) % 4
-                    moved = jnp.where(
-                        group == 0, rl(lh[4, c], -16 * (h * 4 + mu)), rl(l[pair, c, h], 16)
-                    )
-                    terms.append(moved)
+                    moved = rl(l[pair, c, h], 16) if mu == 1 else v[pair, c, h]
+                    halo = rl(lh[4, c], -16 * (h * 4 + mu))
+                    terms.append(jnp.where(group == 0, halo, moved))
                 staple[mu, c, h] = total(terms)
 
     def forces_z(h, carry):
-        forces(1, h, lambda c: staple[1, c, h])
+        forces(jnp.int32(1), h, lambda c: staple[1, c, h])
         return carry
 
     lax.fori_loop(0, 2, forces_z, 0)
@@ -466,12 +505,7 @@
     put_far(3, step_z(1))
     for c in range(FULL):
         for h in range(2):
-            field = hb[2 + h, c]
-            near[2 + h, c] = jnp.where(
-                zrow == 0,
-                rs(field, -1),
-                jnp.where(zrow == 2, rs(field, 1), jnp.where(zrow == 3, rs(field, 2), field)),
-            )
+            near[2 + h, c] = spread_z(hb[2 + h, c])
     lax.fori_loop(2, 4, faces, 0)
     for c in range(FULL):
         for h in range(2):
@@ -511,17 +545,19 @@
             pairs,
             vmem(6, 9, 2),
             vmem(5, ROWS2),
-            vmem(5, ROWS2),
+            vmem(5, FULL),
             vmem(6, 2),
             vmem(5, FULL),
             vmem(5, FULL),
             vmem(6, 2),
+            vmem(5, FULL),
+            vmem(5, FULL),
+            vmem(5, FULL),
             vmem(5, FULL),
             vmem(5, FULL),
             vmem(5, FULL),
             vmem(4, FULL, 2),
             vmem(4, FULL, 2),
-            vmem(4, 9, 2),
             pltpu.SemaphoreType.DMA((4,)),
             pltpu.SemaphoreType.DMA((12,)),
             pltpu.SemaphoreType.DMA((12,)),

time: 18.7 us -> 18 us (0.963)
  Pallas kernels: 17.8 us -> 17.1 us
    pallas_call x1, Pallas kernels: 17.8 us -> 17.1 us  [per_device(): pl.pallas_call(kernel, out_shape=jax.ShapeDtypeStruct(shape, jnp.float32)...]
where the time goes in v4:
time: 18 us; the launch traced here: 17.9 us
  Pallas kernels  17.1 us (95%)
  local copies, waits for them, and re-layouts  0.82 us (5%)
    pallas_call x1, Pallas kernels, per_device(): pl.pallas_call(kernel, out_shape=jax.ShapeDtypeStruct(shape, jnp.float32)...  17.1 us
    unnamed x1, local copies, waits for them, and re-layouts  0.82 us

profile of v4, /device:TPU:1, one launch (start us, length us, event | category | flops | bytes accessed | tf_op | source)
XLA Modules:
  0.0 17.9 jit_solution(5827378697078779633)
XLA Ops:
  0.0 17.1 %force.1 = f32[4,2,3,3,2,8,128]{6,5,4,3,2,1,0:T(8,128)S(1)} custom-call(f32[4,2,3,3,2,8,128]{6,5,4,3,2,1,0:T(8,128)} %bitcast.3), custom_call_target="tpu_custom_call" | custom-call | tf_op jit(solution)/shard_map/force/pallas_call | solution.py:536
  17.1 0.8 %copy.3 = f32[4,2,3,3,4,4,128]{6,5,4,3,2,1,0:T(4,128)} copy(f32[4,2,3,3,4,4,128]{6,5,4,3,2,1,0:T(4,128)S(1)} %bitcast.2) | data formatting | bytes 1179648

commit v5 on v4

--- a/solution.py
+++ b/solution.py
@@ -125,7 +125,7 @@
 
 def kernel(
     x_hbm, o, u, v, p, l, a,
-    sf, sb, sc, hf, hb, hc, far, near, lh, own, pf, lf, staple, below,
+    sf, sb, sc, hf, hb, hc, far, near, lh, own, pf, lf, staple,
     in_sem, send_sem, recv_sem, ready,
 ):
     me = {axis: lax.axis_index(axis) for axis in AXES}
@@ -141,12 +141,11 @@
 
     barrier = pltpu.get_barrier_semaphore()
     targets = [at((d, step)) for d in range(3) for step in (-1, 1)]
-    for target in targets:
-        pl.semaphore_signal(barrier, inc=1, device_id=target, device_id_type=MESH)
-
     loads = [pltpu.make_async_copy(x_hbm.at[d], u.at[d], in_sem.at[d]) for d in range(4)]
     for load in loads:
         load.start()
+    for target in targets:
+        pl.semaphore_signal(barrier, inc=1, device_id=target, device_id_type=MESH)
     for load in loads:
         load.wait()
 
@@ -166,7 +165,7 @@
     next_x = lax.rem(row16 + 112, 128) + lax.rem(xcol + 1, 16)
     time_row = lax.rem(lane + jnp.where(low, 32, 96), 128)
 
-    for c in range(FULL):
+    def pack_tz(c):
         for pair in range(2):
             even, odd = 2 * pair, 2 * pair + 1
             sb[pair, c] = jnp.where(low, rs(link(even, c, 1), 4), link(odd, c, 1))
@@ -182,6 +181,8 @@
                 for k in range(1, 4):
                     first = jnp.where(zrow == k, rs(link(k, c, h), k), first)
                 sf[2 + h, c] = first
+
+    def pack_y(c):
         last = rl(link(0, c, 0), -112)
         for g in range(1, 8):
             last = jnp.where(group == g, rl(link(g % 4, c, g // 4), 16 * (g - 7)), last)
@@ -191,6 +192,10 @@
             for g in range(1, 8):
                 first = jnp.where(group == g, rl(link(g % 4, c, g // 4), 16 * g), first)
             sf[4, c] = first
+
+    for c in range(ROWS2):
+        pack_tz(c)
+        pack_y(c)
 
     def merged(items):
         out = items[0][1]
@@ -252,6 +257,9 @@
         pl.semaphore_wait(ready.at[n], 1)
         for m in through:
             corner[m].start()
+    for c in range(ROWS2, FULL):
+        pack_tz(c)
+        pack_y(c)
 
     def ahead_x(field):
         return pick(field, to_next)
@@ -380,42 +388,95 @@
     lax.fori_loop(0, 4, plaquettes, 0)
     lax.fori_loop(10, 12, plaquettes, 0)
 
-    def step_t0(c):
-        return jnp.where(sub == 7, rs(hc[0, c // 6], 7 - c % 6), rs(hb[0, c], 3))
-
-    def step_t1(c):
+    for c in range(FULL):
+        for mu in range(4):
+            for h in range(2):
+                terms = []
+                if mu != 3:
+                    terms.append(v[mu * 3 + 2 - mu, c, h])
+                if mu != 0:
+                    pair = mu * 3 + 3 - mu
+                    turned = rs(l[pair, c, 0], 4)
+                    if h == 0:
+                        terms.append(jnp.where(low, 0.0, turned))
+                    else:
+                        terms.append(jnp.where(low, turned, rs(l[pair, c, 1], 4)))
+                if mu != 1:
+                    pair = mu * 3 + (0 - mu) % 4
+                    terms.append(jnp.where(zrow == 0, 0.0, rs(l[pair, c, h], 1)))
+                if mu != 2:
+                    pair = mu * 3 + (1 - mu) % 4
+                    moved = rl(l[pair, c, h], 16) if mu == 1 else v[pair, c, h]
+                    terms.append(jnp.where(group == 0, 0.0, moved))
+                staple[mu, c, h] = total(terms)
+
+    for copy in (back_faces[2], back_faces[0], back_faces[1]):
+        copy.wait_recv()
+    for k in range(5):
+        complete(hb, k)
+    for c in range(FULL):
         field = hb[0, c]
+        both = jnp.where(low, field, rs(field, 4))
+        near[0, c] = both
+        near[1, c] = both
+        for h in range(2):
+            near[2 + h, c] = spread_z(hb[2 + h, c])
+        near[4, c] = pick(hb[4, c], own_row)
+    for c in range(ROWS2):
+        field = hb[0, c]
+        far[0, c] = rs(field, 3)
+        far[1, c] = jnp.where(low, rl(field, -16), ahead_x(rs(field, 4)))
+        for h in range(2):
+            field = hb[2 + h, c]
+            along_t = rs(field, 3)
+            if h == 0:
+                along_t = jnp.where(low, along_t, rs(hb[3, c], 3))
+            far[2 + h, c] = jnp.where(
+                zrow == 0,
+                along_t,
+                jnp.where(zrow == 3, ahead_x(rs(field, 2)), rl(rs(field, 1), -16)),
+            )
+        field = hb[4, c]
+        along_t = pick(rs(field, 4), time_row)
+        along_z = rl(rs(field, -1), -16)
+        along_x = pick(field, next_x)
+        far[4, c] = jnp.where(slot == 0, along_t, jnp.where(slot == 3, along_x, along_z))
+
+    for copy in corner:
+        copy.wait_recv()
+
+    def edge_t0(c):
+        return jnp.where(sub == 7, rs(hc[0, c // 6], 7 - c % 6), far[0, c])
+
+    def edge_t1(c):
         edge = rl(rs(hc[1, c // 6], 4), 16 * (7 - c % 6))
-        return jnp.where(
-            low, jnp.where(group == 7, edge, rl(field, -16)), ahead_x(rs(field, 4))
-        )
-
-    def step_z(h):
-        def step(c):
-            field = hb[2 + h, c]
-            if h == 0:
-                along_t = jnp.where(low, rs(field, 3), rs(hb[3, c], 3))
-            else:
-                along_t = jnp.where(low, rs(field, 3), rs(hc[2, c // 6], 4 - c % 6))
+        return jnp.where(low & (group == 7), edge, far[1, c])
+
+    def edge_z(h):
+        def edge_of(c):
             edge = rl(rs(hc[3, h], 2 - c // 6), 16 * (7 - c % 6))
-            along_y = jnp.where(group == 7, edge, rl(rs(field, 1), -16))
-            along_x = ahead_x(rs(field, 2))
-            return jnp.where(zrow == 0, along_t, jnp.where(zrow == 3, along_x, along_y))
-
-        return step
-
-    def step_y(c):
-        field = hb[4, c]
-        turned = rs(field, 4)
-        edge = rs(rl(hc[4, c // 6], 16 * (4 - c % 6)), 4)
-        along_t = jnp.where((group == 4) & (sub >= 4), edge, pick(turned, time_row))
+            out = jnp.where((group == 7) & (zrow == 2), edge, far[2 + h, c])
+            if h == 1:
+                out = jnp.where(sub == 4, rs(hc[2, c // 6], 4 - c % 6), out)
+            return out
+
+        return edge_of
+
+    def edge_y(c):
+        along_t = rs(rl(hc[4, c // 6], 16 * (4 - c % 6)), 4)
         edge0 = rs(rl(hc[5, 0], 16 * (1 - c % 6)), 3 - c // 6)
         edge1 = rs(rl(hc[5, 1], 16 * (5 - c % 6)), 3 - c // 6)
-        along_z = jnp.where(
-            zrow == 3, jnp.where(group == 1, edge0, edge1), rl(rs(field, -1), -16)
-        )
-        along_x = pick(field, next_x)
-        return jnp.where(slot == 0, along_t, jnp.where(slot == 3, along_x, along_z))
+        out = jnp.where((group == 4) & (sub >= 4), along_t, far[4, c])
+        out = jnp.where((group == 1) & (zrow == 3), edge0, out)
+        return jnp.where((group == 5) & (zrow == 3), edge1, out)
+
+    for k, edge in enumerate((edge_t0, edge_t1, edge_z(0), edge_z(1), edge_y)):
+        m = gather(edge, 2)
+
+        def put(c, value):
+            far[k, c] = value
+
+        scatter(put, m + [third_row(m)])
 
     def faces(k, carry):
         prod = mul_nn(gather(lambda c: hb[k, c]), gather(lambda c: far[k, c]))
@@ -426,16 +487,24 @@
         scatter(put, mul_hn(prod, gather(lambda c: near[k, c])))
         return carry
 
-    def put_far(k, step):
-        m = gather(step, 2)
-
-        def put(c, value):
-            far[k, c] = value
-
-        scatter(put, m + [third_row(m)])
-
-    def forces(mu, h, entry):
-        w = anti(mul_nn(gather(lambda c: link(mu, c, h)), gather(entry)))
+    lax.fori_loop(0, 5, faces, 0)
+    for c in range(FULL):
+        for mu in range(4):
+            for h in range(2):
+                out = staple[mu, c, h]
+                if mu != 0 and h == 0:
+                    halo = lh[mu // 2, c]
+                    out = out + jnp.where(low, rs(halo, 4) if mu % 2 else halo, 0.0)
+                if mu != 1:
+                    out = out + jnp.where(zrow == 0, rs(lh[2 + h, c], -mu), 0.0)
+                if mu != 2:
+                    halo = rl(lh[4, c], -16 * (h * 4 + mu))
+                    out = out + jnp.where(group == 0, halo, 0.0)
+                staple[mu, c, h] = out
+
+    def forces(n, carry):
+        mu, h = lax.div(n, 2), lax.rem(n, 2)
+        w = anti(mul_nn(gather(lambda c: link(mu, c, h)), gather(lambda c: staple[mu, c, h])))
         prev, other = lax.rem(mu + 3, 4), 4 + lax.rem(mu, 2)
         sign = 1.0 - 2.0 * lax.div(mu, 2).astype(jnp.float32)
         nine = [
@@ -453,75 +522,9 @@
                 o[mu, 1, i, j, h] = im
                 o[mu, 1, j, i, h] = im
                 k += 2
-
-    for copy in (back_faces[0], back_faces[2], corner[0], corner[1], corner[4], corner[5]):
-        copy.wait_recv()
-    for k in (0, 1, 4):
-        complete(hb, k)
-    put_far(0, step_t0)
-    put_far(1, step_t1)
-    put_far(4, step_y)
-    for c in range(FULL):
-        field = hb[0, c]
-        both = jnp.where(low, field, rs(field, 4))
-        near[0, c] = both
-        near[1, c] = both
-        field = hb[4, c]
-        near[4, c] = pick(field, own_row)
-    lax.fori_loop(0, 3, lambda k, carry: faces(k + lax.div(k, 2) * 2, carry), 0)
-    for c in range(FULL):
-        for mu in range(4):
-            for h in range(2):
-                terms = []
-                if mu != 3:
-                    terms.append(v[mu * 3 + 2 - mu, c, h])
-                if mu != 0:
-                    pair = mu * 3 + 3 - mu
-                    turned = rs(l[pair, c, 0], 4)
-                    if h == 0:
-                        halo = lh[mu // 2, c]
-                        moved = jnp.where(low, rs(halo, 4) if mu % 2 else halo, turned)
-                    else:
-                        moved = jnp.where(low, turned, rs(l[pair, c, 1], 4))
-                    terms.append(moved)
-                if mu != 2:
-                    pair = mu * 3 + (1 - mu) % 4
-                    moved = rl(l[pair, c, h], 16) if mu == 1 else v[pair, c, h]
-                    halo = rl(lh[4, c], -16 * (h * 4 + mu))
-                    terms.append(jnp.where(group == 0, halo, moved))
-                staple[mu, c, h] = total(terms)
-
-    def forces_z(h, carry):
-        forces(jnp.int32(1), h, lambda c: staple[1, c, h])
         return carry
 
-    lax.fori_loop(0, 2, forces_z, 0)
-
-    for copy in (back_faces[1], corner[2], corner[3]):
-        copy.wait_recv()
-    for k in (2, 3):
-        complete(hb, k)
-    put_far(2, step_z(0))
-    put_far(3, step_z(1))
-    for c in range(FULL):
-        for h in range(2):
-            near[2 + h, c] = spread_z(hb[2 + h, c])
-    lax.fori_loop(2, 4, faces, 0)
-    for c in range(FULL):
-        for h in range(2):
-            for mu in (0, 2, 3):
-                pair = mu * 3 + (0 - mu) % 4
-                below[mu, c, h] = jnp.where(
-                    zrow == 0, rs(lh[2 + h, c], -mu), rs(l[pair, c, h], 1)
-                )
-
-    def forces_rest(n, carry):
-        m, h = lax.div(n, 2), lax.rem(n, 2)
-        mu = m + lax.div(m + 1, 2)
-        forces(mu, h, lambda c: staple[mu, c, h] + below[mu, c, h])
-        return carry
-
-    lax.fori_loop(0, 6, forces_rest, 0)
+    lax.fori_loop(0, 8, forces, 0)
     for copy in ahead_faces + back_faces + corner:
         copy.wait_send()
 
@@ -557,7 +560,6 @@
             vmem(5, FULL),
             vmem(5, FULL),
             vmem(4, FULL, 2),
-            vmem(4, FULL, 2),
             pltpu.SemaphoreType.DMA((4,)),
             pltpu.SemaphoreType.DMA((12,)),
             pltpu.SemaphoreType.DMA((12,)),

time: 18 us -> 17.7 us (0.983)
  Pallas kernels: 17.1 us -> 16.8 us
    pallas_call x1, Pallas kernels: 17.1 us -> 16.8 us  [per_device(): pl.pallas_call(kernel, out_shape=jax.ShapeDtypeStruct(shape, jnp.float32)...]
where the time goes in v5:
time: 17.7 us; the launch traced here: 17.6 us
  Pallas kernels  16.8 us (95%)
  local copies, waits for them, and re-layouts  0.82 us (5%)
    pallas_call x1, Pallas kernels, per_device(): pl.pallas_call(kernel, out_shape=jax.ShapeDtypeStruct(shape, jnp.float32)...  16.8 us
    unnamed x1, local copies, waits for them, and re-layouts  0.82 us

profile of v5, /device:TPU:1, one launch (start us, length us, event | category | flops | bytes accessed | tf_op | source)
XLA Modules:
  0.0 17.6 jit_solution(5842047608004582139)
XLA Ops:
  0.0 16.8 %force.1 = f32[4,2,3,3,2,8,128]{6,5,4,3,2,1,0:T(8,128)S(1)} custom-call(f32[4,2,3,3,2,8,128]{6,5,4,3,2,1,0:T(8,128)} %bitcast.3), custom_call_target="tpu_custom_call" | custom-call | tf_op jit(solution)/shard_map/force/pallas_call | solution.py:539
  16.8 0.8 %copy.3 = f32[4,2,3,3,4,4,128]{6,5,4,3,2,1,0:T(4,128)} copy(f32[4,2,3,3,4,4,128]{6,5,4,3,2,1,0:T(4,128)S(1)} %bitcast.2) | data formatting | bytes 1179648

commit v6 on v5

--- a/solution.py
+++ b/solution.py
@@ -247,13 +247,13 @@
         send(3 + d, sb.at[tiles[d], two], hb.at[tiles[d], two], at((d, 1))) for d in range(3)
     ]
     pl.semaphore_wait(barrier, len(targets))
-    words = ((0, -1), (0, 1), (2, -1), (2, 1))
+    words = ((0, -1), (0, 1), (1, -1), (1, 1))
     for n, word in enumerate(words):
         pl.semaphore_signal(ready.at[n], inc=1, device_id=at(word), device_id_type=MESH)
     for d in (1, 0, 2):
         back_faces[d].start()
         ahead_faces[d].start()
-    for n, through in enumerate(((0,), (2,), (4, 5), (1, 3))):
+    for n, through in enumerate(((0, 1), (2, 4), (3,), (5,))):
         pl.semaphore_wait(ready.at[n], 1)
         for m in through:
             corner[m].start()
@@ -364,16 +364,16 @@
             v[j, c, 1] = jnp.where(
                 low, rs(link(nu, c, 1), 4), halo if nu % 2 else rs(halo, 4)
             )
-    lax.fori_loop(0, 3, lambda j, carry: products(2 * j + 1, carry), 0)
+    lax.fori_loop(0, 3, lambda j, carry: products(2 * j + 1, carry), 0, unroll=3)
     for c in range(FULL):
         v[2, c, 1] = pick(l[2, c, 1], to_last)
         v[1, c, 1] = rl(l[1, c, 1], 16)
-    lax.fori_loop(4, 10, plaquettes, 0)
+    lax.fori_loop(4, 10, plaquettes, 0, unroll=2)
 
     ahead_faces[1].wait_recv()
     for k in range(2, 4):
         complete(hf, k)
-    lax.fori_loop(2, 4, last_products, 0)
+    lax.fori_loop(2, 4, last_products, 0, unroll=2)
     for c in range(FULL):
         for j in range(3):
             nu = (2 + j) % 4
@@ -385,8 +385,8 @@
                     l[3 + j, c, h] = jnp.where(
                         zrow == 3, rs(lf[2 + h, c], 3 - nu), l[3 + j, c, h]
                     )
-    lax.fori_loop(0, 4, plaquettes, 0)
-    lax.fori_loop(10, 12, plaquettes, 0)
+    lax.fori_loop(0, 4, plaquettes, 0, unroll=2)
+    lax.fori_loop(10, 12, plaquettes, 0, unroll=2)
 
     for c in range(FULL):
         for mu in range(4):
@@ -487,7 +487,7 @@
         scatter(put, mul_hn(prod, gather(lambda c: near[k, c])))
         return carry
 
-    lax.fori_loop(0, 5, faces, 0)
+    lax.fori_loop(0, 5, faces, 0, unroll=5)
     for c in range(FULL):
         for mu in range(4):
             for h in range(2):
@@ -524,7 +524,7 @@
                 k += 2
         return carry
 
-    lax.fori_loop(0, 8, forces, 0)
+    lax.fori_loop(0, 8, forces, 0, unroll=4)
     for copy in ahead_faces + back_faces + corner:
         copy.wait_send()
 

time: 17.7 us -> 17.3 us (0.977)
  Pallas kernels: 16.8 us -> 16.4 us
    pallas_call x1, Pallas kernels: 16.8 us -> 16.4 us  [per_device(): pl.pallas_call(kernel, out_shape=jax.ShapeDtypeStruct(shape, jnp.float32)...]
where the time goes in v6:
time: 17.3 us; the launch traced here: 17.2 us
  Pallas kernels  16.4 us (95%)
  local copies, waits for them, and re-layouts  0.82 us (5%)
    pallas_call x1, Pallas kernels, per_device(): pl.pallas_call(kernel, out_shape=jax.ShapeDtypeStruct(shape, jnp.float32)...  16.4 us
    unnamed x1, local copies, waits for them, and re-layouts  0.82 us

profile of v6, /device:TPU:1, one launch (start us, length us, event | category | flops | bytes accessed | tf_op | source)
XLA Modules:
  0.0 17.2 jit_solution(4115485398854020025)
XLA Ops:
  0.0 16.4 %force.1 = f32[4,2,3,3,2,8,128]{6,5,4,3,2,1,0:T(8,128)S(1)} custom-call(f32[4,2,3,3,2,8,128]{6,5,4,3,2,1,0:T(8,128)} %bitcast.3), custom_call_target="tpu_custom_call" | custom-call | tf_op jit(solution)/shard_map/force/pallas_call | solution.py:539
  16.4 0.8 %copy.3 = f32[4,2,3,3,4,4,128]{6,5,4,3,2,1,0:T(4,128)} copy(f32[4,2,3,3,4,4,128]{6,5,4,3,2,1,0:T(4,128)S(1)} %bitcast.2) | data formatting | bytes 1179648

commit v7 on v6

--- a/solution.py
+++ b/solution.py
@@ -339,6 +339,31 @@
             v[6, c, h] = pick(l[6, c, h], to_last)
             v[11, c, h] = rl(l[11, c, h], 16)
 
+    def own_staples(mu, c, h):
+        terms = []
+        if mu != 3:
+            terms.append(v[mu * 3 + 2 - mu, c, h])
+        if mu != 0:
+            pair = mu * 3 + 3 - mu
+            turned = rs(l[pair, c, 0], 4)
+            if h == 0:
+                terms.append(jnp.where(low, 0.0, turned))
+            else:
+                terms.append(jnp.where(low, turned, rs(l[pair, c, 1], 4)))
+        if mu != 1:
+            pair = mu * 3 + (0 - mu) % 4
+            terms.append(jnp.where(zrow == 0, 0.0, rs(l[pair, c, h], 1)))
+        if mu != 2:
+            pair = mu * 3 + (1 - mu) % 4
+            moved = rl(l[pair, c, h], 16) if mu == 1 else v[pair, c, h]
+            terms.append(jnp.where(group == 0, 0.0, moved))
+        return total(terms)
+
+    for c in range(FULL):
+        staple[0, c, 0] = own_staples(0, c, 0)
+        for h in range(2):
+            staple[3, c, h] = own_staples(3, c, h)
+
     ahead_faces[2].wait_recv()
     complete(hf, 4)
     lax.fori_loop(4, 5, last_products, 0)
@@ -368,7 +393,7 @@
     for c in range(FULL):
         v[2, c, 1] = pick(l[2, c, 1], to_last)
         v[1, c, 1] = rl(l[1, c, 1], 16)
-    lax.fori_loop(4, 10, plaquettes, 0, unroll=2)
+    lax.fori_loop(4, 10, plaquettes, 0, unroll=3)
 
     ahead_faces[1].wait_recv()
     for k in range(2, 4):
@@ -385,30 +410,13 @@
                     l[3 + j, c, h] = jnp.where(
                         zrow == 3, rs(lf[2 + h, c], 3 - nu), l[3 + j, c, h]
                     )
-    lax.fori_loop(0, 4, plaquettes, 0, unroll=2)
+    lax.fori_loop(0, 4, plaquettes, 0, unroll=4)
     lax.fori_loop(10, 12, plaquettes, 0, unroll=2)
 
     for c in range(FULL):
-        for mu in range(4):
-            for h in range(2):
-                terms = []
-                if mu != 3:
-                    terms.append(v[mu * 3 + 2 - mu, c, h])
-                if mu != 0:
-                    pair = mu * 3 + 3 - mu
-                    turned = rs(l[pair, c, 0], 4)
-                    if h == 0:
-                        terms.append(jnp.where(low, 0.0, turned))
-                    else:
-                        terms.append(jnp.where(low, turned, rs(l[pair, c, 1], 4)))
-                if mu != 1:
-                    pair = mu * 3 + (0 - mu) % 4
-                    terms.append(jnp.where(zrow == 0, 0.0, rs(l[pair, c, h], 1)))
-                if mu != 2:
-                    pair = mu * 3 + (1 - mu) % 4
-                    moved = rl(l[pair, c, h], 16) if mu == 1 else v[pair, c, h]
-                    terms.append(jnp.where(group == 0, 0.0, moved))
-                staple[mu, c, h] = total(terms)
+        for mu in range(3):
+            for h in range(0 if mu else 1, 2):
+                staple[mu, c, h] = own_staples(mu, c, h)
 
     for copy in (back_faces[2], back_faces[0], back_faces[1]):
         copy.wait_recv()
@@ -524,7 +532,7 @@
                 k += 2
         return carry
 
-    lax.fori_loop(0, 8, forces, 0, unroll=4)
+    lax.fori_loop(0, 8, forces, 0, unroll=8)
     for copy in ahead_faces + back_faces + corner:
         copy.wait_send()
 

time: 17.3 us -> 17.3 us (level)
  no operation moved by 1% of the time
where the time goes in v7:
time: 17.3 us
  Pallas kernels  16.4 us (95%)
  local copies, waits for them, and re-layouts  0.82 us (5%)
    pallas_call x1, Pallas kernels, per_device(): pl.pallas_call(kernel, out_shape=jax.ShapeDtypeStruct(shape, jnp.float32)...  16.4 us
    unnamed x1, local copies, waits for them, and re-layouts  0.82 us

profile of v7, /device:TPU:1, one launch (start us, length us, event | category | flops | bytes accessed | tf_op | source)
XLA Modules:
  0.0 17.3 jit_solution(17400367103047154296)
XLA Ops:
  0.0 16.4 %force.1 = f32[4,2,3,3,2,8,128]{6,5,4,3,2,1,0:T(8,128)S(1)} custom-call(f32[4,2,3,3,2,8,128]{6,5,4,3,2,1,0:T(8,128)} %bitcast.3), custom_call_target="tpu_custom_call" | custom-call | tf_op jit(solution)/shard_map/force/pallas_call | solution.py:547
  16.4 0.8 %copy.3 = f32[4,2,3,3,4,4,128]{6,5,4,3,2,1,0:T(4,128)} copy(f32[4,2,3,3,4,4,128]{6,5,4,3,2,1,0:T(4,128)S(1)} %bitcast.2) | data formatting | bytes 1179648
